TPU v7x, 16 devices: a whole 2x2x2 slice. The times are simulated.
16 devices in a mesh: dp: 16 (over z, y, x, core).
Axes of the slice: x: 2, y: 2, z: 2, core: 2. Of those that a mesh axis runs over, the one named last changes fastest.
Arguments:
- user_x: float32 [8192, 384], P('dp')
- item_x: float32 [8192, 384], P('dp')
- item_id: int32 [8192], P('dp')
- log_q: float32 [8192], P('dp')
- user_w1: float32 [384, 1536], replicated
- user_w2: float32 [1536, 384], replicated
- user_w3: float32 [384, 384], replicated
- item_w1: float32 [384, 1536], replicated
- item_w2: float32 [1536, 384], replicated
- item_w3: float32 [384, 384], replicated
Outputs:
- output 1: float32 [], replicated
- output 2: float32 [384, 1536], replicated
- output 3: float32 [1536, 384], replicated
- output 4: float32 [384, 384], replicated
- output 5: float32 [384, 1536], replicated
- output 6: float32 [1536, 384], replicated
- output 7: float32 [384, 384], replicated
All inputs are finite; a program needn't handle non-finite values.
Results may differ from a plain program's by a relative error of at most 0.0042753.
Values are sent between devices in bfloat16 or wider.
A program may use at most 1 GiB of HBM per device.

v0:
```python
import jax
import jax.numpy as jnp
from jax import lax
from jax.sharding import PartitionSpec as P

value_a11 = 0.05
INV_TEMP = 1.0 / value_a11
NORM_EPS = 1e-6
ROW_DIMS = (((0,), (0,)), ((), ()))
COL_DIMS = (((1,), (1,)), ((), ()))


def tower_forward(inputs, w_one, w_two, w_three):
    x_half = inputs.astype(jnp.bfloat16)
    pre_one = jnp.dot(x_half, w_one, preferred_element_type=jnp.float32)
    act_one = jnp.maximum(pre_one, 0.0).astype(jnp.bfloat16)
    pre_two = jnp.dot(act_one, w_two, preferred_element_type=jnp.float32)
    act_two = jnp.maximum(pre_two, 0.0).astype(jnp.bfloat16)
    raw_out = jnp.dot(act_two, w_three, preferred_element_type=jnp.float32)
    inv_norm = lax.rsqrt(jnp.sum(raw_out * raw_out, axis=1, keepdims=True) + NORM_EPS)
    return (x_half, pre_one, act_one, pre_two, act_two, raw_out * inv_norm, inv_norm)


def tower_backward(saved, w_two, w_three, grad_unit):
    x_half, pre_one, act_one, pre_two, act_two, unit_out, inv_norm = saved
    grad_raw = inv_norm * (grad_unit - unit_out * jnp.sum(unit_out * grad_unit, axis=1, keepdims=True))
    grad_raw_h = grad_raw.astype(jnp.bfloat16)
    grad_three = lax.dot_general(act_two, grad_raw_h, ROW_DIMS, preferred_element_type=jnp.float32)
    grad_act_two = lax.dot_general(grad_raw_h, w_three, COL_DIMS, preferred_element_type=jnp.float32)
    grad_pre_two = jnp.where(pre_two > 0.0, grad_act_two, 0.0).astype(jnp.bfloat16)
    grad_two = lax.dot_general(act_one, grad_pre_two, ROW_DIMS, preferred_element_type=jnp.float32)
    grad_act_one = lax.dot_general(grad_pre_two, w_two, COL_DIMS, preferred_element_type=jnp.float32)
    grad_pre_one = jnp.where(pre_one > 0.0, grad_act_one, 0.0).astype(jnp.bfloat16)
    grad_one = lax.dot_general(x_half, grad_pre_one, ROW_DIMS, preferred_element_type=jnp.float32)
    return (grad_one, grad_two, grad_three)


def solution(mesh):
    def device_step(user_x, item_x, item_id, log_q, user_w1, user_w2, user_w3, item_w1, item_w2, item_w3):
        user_ws = (user_w1.astype(jnp.bfloat16), user_w2.astype(jnp.bfloat16), user_w3.astype(jnp.bfloat16))
        item_ws = (item_w1.astype(jnp.bfloat16), item_w2.astype(jnp.bfloat16), item_w3.astype(jnp.bfloat16))
        user_saved = tower_forward(user_x, user_ws[0], user_ws[1], user_ws[2])
        item_saved = tower_forward(item_x, item_ws[0], item_ws[1], item_ws[2])
        user_half = user_saved[5].astype(jnp.bfloat16)
        item_half = item_saved[5].astype(jnp.bfloat16)
        item_all = lax.all_gather(item_half, 'dp', axis=0, tiled=True)
        logq_all = lax.all_gather(log_q, 'dp', axis=0, tiled=True)
        id_all = lax.all_gather(item_id, 'dp', axis=0, tiled=True)
        local_rows = user_x.shape[0]
        batch = item_all.shape[0]
        query_pos = lax.axis_index('dp') * local_rows + jnp.arange(local_rows)
        cand_pos = jnp.arange(batch)
        is_self = query_pos[:, None] == cand_pos[None, :]
        dropped = jnp.logical_and(item_id[:, None] == id_all[None, :], jnp.logical_not(is_self))
        raw = lax.dot_general(user_half, item_all, COL_DIMS, preferred_element_type=jnp.float32) * INV_TEMP - logq_all[None, :]
        scores = jnp.where(dropped, -jnp.inf, raw)
        row_max = jnp.max(scores, axis=1, keepdims=True)
        exp_scores = jnp.exp(scores - row_max)
        row_total = jnp.sum(exp_scores, axis=1, keepdims=True)
        log_norm = row_max[:, 0] + jnp.log(row_total[:, 0])
        pos_score = jnp.sum(user_half.astype(jnp.float32) * item_half.astype(jnp.float32), axis=1) * INV_TEMP - log_q
        softmax_rows = exp_scores / row_total
        grad_scores = (jnp.where(is_self, softmax_rows - 1.0, softmax_rows) / batch).astype(jnp.bfloat16)
        grad_user = jnp.dot(grad_scores, item_all, preferred_element_type=jnp.float32) * INV_TEMP
        item_part = lax.dot_general(grad_scores, user_half, ROW_DIMS, preferred_element_type=jnp.float32) * INV_TEMP
        grad_item = lax.psum_scatter(item_part, 'dp', scatter_dimension=0, tiled=True)
        user_grads = tower_backward(user_saved, user_ws[1], user_ws[2], grad_user)
        item_grads = tower_backward(item_saved, item_ws[1], item_ws[2], grad_item)
        totals = lax.psum((jnp.sum(log_norm - pos_score),) + user_grads + item_grads, 'dp')
        return (totals[0] / batch,) + tuple(totals[1:])

    batch_spec = P('dp', None)
    vec_spec = P('dp')
    whole = P()
    return jax.shard_map(device_step, mesh=mesh,
                         in_specs=(batch_spec, batch_spec, vec_spec, vec_spec, whole, whole, whole, whole, whole, whole),
                         out_specs=(whole, whole, whole, whole, whole, whole, whole), check_vma=False)
```

profile of v0, /device:TPU:0, one launch (start us, length us, event | category | flops | bytes accessed | tf_op | source)
XLA Modules:
  0.0 367.5 jit_solution(13368543213556726)
XLA Ops:
  7.2 3.0 fusion.11
  18.9 1.5 multiply_reduce_fusion.2
  20.6 15.2 %all-gather.1 = f32[16,1,512]{2,1,0:T(1,128)} all-gather(f32[1,1,512]{2,1,0:T(1,128)} %bitcast.24), channel_id=1, replica_groups=mesh['dp'=16] {'dp'}, dimensions={0}, use_global_device_ids=true | all-gather | bytes 34816 | tf_op jit(solution)/shard_map/all_gather | solution.py:47
  35.8 12.0 %all-gather = s32[16,1,512]{2,1,0:T(1,128)} all-gather(s32[1,1,512]{2,1,0:T(1,128)} %bitcast.25), channel_id=1, replica_groups=mesh['dp'=16] {'dp'}, dimensions={0}, use_global_device_ids=true | all-gather | bytes 34816 | tf_op jit(solution)/shard_map/all_gather | solution.py:48
  47.8 21.2 %all-gather.4.cloned.1.call-done = bf16[8192,384]{0,1:T(8,128)(2,1)} async-done(((bf16[512,384]{0,1:T(8,128)(2,1)}), bf16[8192,384]{0,1:T(8,128)(2,1)}) %all-gather.4.cloned.1.call-update) | async-done | bytes 6291472 | tf_op jit(solution)/shard_map/all_gather | solution.py:46
  69.0 16.3 %fusion.45 = (f32[512]{0:T(512)S(1)}, f32[512,8192]{1,0:T(8,128)}) fusion(f32[8192]{0:T(1024)} %bitcast.22, bf16[512,384]{0,1:T(8,128)(2,1)S(1)} %get-tuple-element.28, bf16[8192,384]{0,1:T(8,128)(2,1)} %all-gather.4.cloned.1.call-done, s32[512]{0:T(512)S(1)} %iota_add_fusion, s32[8192]{0:T(1024)} %bitcast.23, s32[512]{0:T(512)} %param.12), kind=kOutput, calls=%fused_computation.72 | convolution fusion | flops 3254779392 | bytes 23533568 | tf_op jit(solution)/shard_map/dot_general | solution.py:55
  85.3 8.1 %fusion.4 = f32[512]{0:T(512)S(1)} fusion(f32[512,8192]{1,0:T(8,128)} %get-tuple-element.35, f32[512]{0:T(512)S(1)} %get-tuple-element.34), kind=kLoop, calls=%fused_computation.8 | loop fusion | flops 8388096 | bytes 16781312 | tf_op jit(solution)/shard_map/reduce_sum | solution.py:59
  93.4 8.7 %fusion.1 = bf16[512,8192]{1,0:T(8,128)(2,1)S(1)} fusion(f32[512,8192]{1,0:T(8,128)} %get-tuple-element.35, f32[512]{0:T(512)S(1)} %fusion.4, f32[512]{0:T(512)S(1)} %get-tuple-element.34, s32[512]{0:T(512)S(1)} %copy-done.23), kind=kLoop, calls=%fused_computation.2 | loop fusion | flops 29360128 | bytes 25171968 | tf_op jit(solution)/shard_map/convert_element_type | solution.py:63
  102.2 3.2 copy-done
  105.4 6.3 %convolution_multiply_fusion = f32[8192,384]{0,1:T(8,128)} fusion(bf16[512,384]{0,1:T(8,128)(2,1)S(1)} %get-tuple-element.28, bf16[512,8192]{1,0:T(8,128)(2,1)S(1)} %fusion.1), kind=kOutput, calls=%fused_computation.9 | convolution fusion | flops 3224371200 | bytes 21364736 | tf_op jit(solution)/shard_map/dot_general | solution.py:65
  112.0 8.9 %multiply_reduce_fusion.1 = (f32[512]{0:T(512)S(1)}, f32[512,384]{0,1:T(8,128)S(1)}) fusion(f32[512,384]{0,1:T(8,128)} %copy-done.10, f32[512]{0:T(512)S(1)} %get-tuple-element.39, bf16[512,8192]{1,0:T(8,128)(2,1)} %copy-done, bf16[8192,384]{0,1:T(8,128)(2,1)} %all-gather.4.cloned.1.call-done), kind=kOutput, calls=%fused_computation.30 | convolution fusion | flops 3222011392 | bytes 16257024 | tf_op jit(solution)/shard_map/dot_general | solution.py:64
  123.2 2.4 fusion.13
  125.7 6.0 %convolution_bitcast_fusion.1 = f32[384,1536]{0,1:T(8,128)} fusion(bf16[512,384]{1,0:T(8,128)(2,1)S(1)} %fusion.7, f32[512,1536]{1,0:T(8,128)} %copy-done.1, f32[1536,384]{1,0:T(8,128)} %param.15, f32[512,384]{1,0:T(8,128)} %param.10), kind=kOutput, calls=%fused_computation.15 | convolution fusion | flops 1211105280 | bytes 9043968 | tf_op jit(solution)/shard_map/dot_general | solution.py:34
  131.7 70.6 %reduce-scatter.2.cloned.1.call-done = f32[512,384]{0,1:T(8,128)} async-done(((f32[8192,384]{0,1:T(8,128)}), f32[512,384]{0,1:T(8,128)}) %reduce-scatter.2.cloned.1.call-update) | async-done | bytes 786448 | tf_op jit(solution)/shard_map/reduce_scatter | solution.py:66
  202.3 1.6 multiply_reduce_fusion
  203.9 1.6 multiply_convert_fusion
  207.2 2.4 fusion.15
  209.6 5.1 %convolution_bitcast_fusion = f32[384,1536]{0,1:T(8,128)} fusion(bf16[512,384]{1,0:T(8,128)(2,1)S(1)} %fusion.8, f32[512,1536]{1,0:T(8,128)S(1)} %fusion.9, f32[1536,384]{1,0:T(8,128)} %param.18, f32[512,384]{1,0:T(8,128)} %param.11), kind=kOutput, calls=%fused_computation.14 | convolution fusion | flops 1211105280 | bytes 9043968 | tf_op jit(solution)/shard_map/dot_general | solution.py:34
  216.0 32.7 %psum.49 = f32[]{:T(128)} all-reduce(f32[]{:T(128)} %subtract_reduce_fusion), channel_id=1, replica_groups=mesh['dp'=16] {'dp'}, use_global_device_ids=true, to_apply=%region_6.7 | all-reduce | flops 1 | bytes 8 | tf_op jit(solution)/shard_map/psum | solution.py:69
  249.3 98.9 %all-reduce.3.cloned.1.call-done = (f32[384,1536]{0,1:T(8,128)}, f32[1536,384]{1,0:T(8,128)}, f32[384,384]{1,0:T(8,128)}, f32[384,1536]{0,1:T(8,128)}, f32[1536,384]{1,0:T(8,128)}, /*index=5*/f32[384,384]{1,0:T(8,128)}) async-done(((f32[384,1536]{0,1:T(8,128)}, f32[1536,384]{1,0:T(8,128)}, f32[384,384]{1,0:T(8,128)}, f32[384,1536]{0,1:T(8,128)}, f32[1536,384]{1,0:T(8,128)}, ...) | async-done | bytes 10616848 | tf_op jit(solution)/shard_map/psum | solution.py:69
  348.3 3.2 copy.21
  351.5 1.9 copy.22
  353.4 3.4 copy.30
  357.6 1.4 copy.32
  (72 shorter events, 15.8 us)
Async XLA Ops:
  7.2 61.8 %all-gather.4.cloned.1.call-start = ((), (), s32[]{:S(2)}) async-start(), calls=%async_computation.1 | async-start | bytes 6684672 | tf_op jit(solution)/shard_map/all_gather | solution.py:46
  7.2 3.1 copy-start.8
  10.3 1.8 copy-start.1
  10.3 1.8 copy-start.16
  10.3 2.6 copy-start.12
  10.3 3.5 copy-start.13
  13.8 4.3 %copy-start.10 = (f32[512,384]{0,1:T(8,128)}, f32[512,384]{0,1:T(8,128)S(1)}, u32[]{:S(2)}) copy-start(f32[512,384]{0,1:T(8,128)S(1)} %get-tuple-element.31) | copy-start | bytes 2359300
  13.8 1.9 copy-start.9
  15.7 1.9 copy-start.18
  20.5 181.8 %reduce-scatter.2.cloned.1.call-start = ((), (), s32[]{:S(2)}) async-start(), calls=%async_computation.2 | async-start | bytes 13369344 | tf_op jit(solution)/shard_map/reduce_scatter | solution.py:66
  47.8 37.6 %copy-start.22 = (s32[512]{0:T(512)}, s32[512]{0:T(512)S(1)}, u32[]{:S(2)}) copy-start(s32[512]{0:T(512)S(1)} %iota_add_fusion) | copy-start | bytes 6148
  85.3 8.1 %copy-start.23 = (s32[512]{0:T(512)S(1)}, s32[512]{0:T(512)}, u32[]{:S(2)}) copy-start(s32[512]{0:T(512)} %copy-done.22) | copy-start | bytes 6148
  102.2 3.2 copy-start
  111.7 236.5 %all-reduce.3.cloned.1.call-start = ((), (), s32[]{:S(2)}) async-start(), calls=%async_computation.3 | async-start | bytes 21233664 | tf_op jit(solution)/shard_map/psum | solution.py:69
  112.0 9.0 %copy-start.11 = (f32[512,384]{0,1:T(8,128)S(1)}, f32[512,384]{0,1:T(8,128)}, u32[]{:S(2)}) copy-start(f32[512,384]{0,1:T(8,128)} %copy-done.10) | copy-start | bytes 2359300
  112.0 9.2 %copy-start.6 = (f32[512,384]{1,0:T(8,128)S(1)}, f32[512,384]{1,0:T(8,128)}, u32[]{:S(2)}) copy-start(f32[512,384]{1,0:T(8,128)} %copy-done.5) | copy-start | bytes 2359300
  120.9 1.5 copy-start.17
  121.0 2.3 copy-start.2
  202.3 3.2 copy-start.4
  202.3 3.2 copy-start.19
  348.3 3.2 copy-start.15
  353.4 3.4 copy-start.21
  353.4 4.2 %copy-start.14 = (f32[1536,384]{1,0:T(8,128)S(1)}, f32[1536,384]{1,0:T(8,128)}, u32[]{:S(2)}) copy-start(f32[1536,384]{1,0:T(8,128)} %get-tuple-element.45) | copy-start | bytes 7077892
  356.8 2.2 copy-start.20
  (5 other events, 4.0 us)
Sparse Core Ops, SparseCore 0:
  20.6 48.3 all-gather.3
  111.9 90.4 reduce-scatter.1
  214.9 133.3 all-reduce.2
where the time goes:
time: 368 us; the launch traced here: 367 us
  waiting for transfers between devices  191 us (52%)
  blocking collectives  59.9 us (16%)
  matrix products  57.7 us (16%)
  other arithmetic  22.4 us (6%)
  local copies, waits for them, and re-layouts  20.6 us (6%)
  between operations  15.8 us (4%)
    psum x1, waiting for transfers between devices, device_step(): lax.psum((jnp.sum(log_norm - pos_score),) + user_grads + item_grads, 'dp')  98.9 us
    reduce_scatter x1, waiting for transfers between devices, device_step(): lax.psum_scatter(item_part, 'dp', scatter_dimension=0, tiled=True)  70.6 us
    psum x1, blocking collectives, device_step(): lax.psum((jnp.sum(log_norm - pos_score),) + user_grads + item_grads, 'dp')  32.7 us
    all_gather x1, waiting for transfers between devices, device_step(): item_all = lax.all_gather(item_half, 'dp', axis=0, tiled=True)  21.2 us
    unnamed x58, local copies, waits for them, and re-layouts  20.6 us
    dot_general x1, matrix products, device_step(): lax.dot_general(user_half, item_all, COL_DIMS, preferred_element_type=jnp...  16.3 us
    all_gather x1, blocking collectives, device_step(): logq_all = lax.all_gather(log_q, 'dp', axis=0, tiled=True)  15.2 us
    all_gather x1, blocking collectives, device_step(): id_all = lax.all_gather(item_id, 'dp', axis=0, tiled=True)  12 us
  transfers between devices with their start and end apart: 3, of which 3 were waited for; matrix products, arithmetic and copies ran while one was open for 5% of the time, Pallas kernels for 0%

commit v1 on v0

v1 whole, which is shorter than its diff:
```python
import jax
import jax.numpy as jnp
from jax import lax
from jax.experimental import pallas as pl
from jax.experimental.pallas import tpu as pltpu
from jax.sharding import PartitionSpec as P

SCALE = 20.0
EPS = 1e-6
NDEV = 16
R = 512
D = 384
H = 1536
B = R * NDEV
BLK = 216
HALF = 8 * BLK
PACK = 2 * HALF
WROWS = 3 * PACK
L = 128
CH = 64
F32, BF16 = jnp.float32, jnp.bfloat16
MESH = pl.DeviceIdType.MESH
NT = (((1,), (1,)), ((), ()))
TN = (((0,), (0,)), ((), ()))
LOWEST = float(jnp.finfo(jnp.float32).min)
V_AG, U_AG = 0, 29
IDS, LQS, STS = 58, 74, 90
AR = (106, 162)
N_SEM = 218
DIMS = (4, 2, 1)


def dot(a, b, dims=(((1,), (0,)), ((), ()))):
    return lax.dot_general(a, b, dims, preferred_element_type=F32)


def kernel(ux, ix, ids_in, lq_in, uw1, uw2, uw3, iw1, iw2, iw3,
           loss, gu1, gu2, gu3, gi1, gi2, gi3,
           S, v_all, u_all, xf, xb, h1, h2, e_ref, inv_ref, w1b, w2b, w3b, da1,
           ids_all, lq_all, st_all, idcol, lqcol, m_ref, l_ref, pos_ref, G, acc, big,
           recv_d, rb1, rb2, rb3, send_sem, recv_sem, loc_sem, out_sem):
    me = lax.axis_index('dp')
    core = lax.rem(me, 2)
    chip = lax.div(me, 2)
    partner = me + 1 - 2 * core

    def flip(m):
        out = 0
        for d in DIMS:
            bit = lax.rem(lax.div(chip, d), 2)
            if isinstance(m, int):
                f = (m // d) % 2
            else:
                f = lax.rem(lax.div(m, d), 2)
            out = out + d * (bit + f - 2 * bit * f)
        return out

    chips = [flip(m) for m in range(8)]

    def nbr(d):
        return chips[d] * 2 + core

    def rc(src, dst, idx, dev):
        return pltpu.make_async_remote_copy(src, dst, send_sem.at[idx], recv_sem.at[idx],
                                            device_id=(dev,), device_id_type=MESH)

    started = []

    def send(src, dst, idx, dev):
        c = rc(src, dst, idx, dev)
        c.start()
        started.append(c)

    def flush():
        for c in started:
            c.wait_send()
        started.clear()

    def arrived(ref, idx):
        rc(ref, ref, idx, partner).wait_recv()

    barrier = pltpu.get_barrier_semaphore()
    for i in range(1, NDEV):
        pl.semaphore_signal(barrier, inc=1, device_id=(lax.rem(me + i, NDEV),), device_id_type=MESH)

    loads = {0: [], 1: []}

    def load(t, src, dst, k):
        c = pltpu.make_async_copy(src, dst, loc_sem.at[t, k])
        c.start()
        loads[t].append(c)

    for t, (xr, w1, w2, w3) in enumerate(((ix, iw1, iw2, iw3), (ux, uw1, uw2, uw3))):
        o = t * WROWS
        load(t, xr, xf.at[t], 0)
        for c in range(12):
            load(t, w1.at[:, pl.ds(L * c, L)], S.at[pl.ds(o + D * c, D), :], 1 + c)
        for c in range(3):
            load(t, w2.at[:, pl.ds(L * c, L)], S.at[pl.ds(o + 4608 + H * c, H), :], 13 + c)
        for c in range(3):
            load(t, w3.at[:, pl.ds(L * c, L)], S.at[pl.ds(o + 9216 + D * c, D), :], 16 + c)

    ids_all[me] = ids_in[...]
    lq_all[me] = lq_in[...]
    idcol[...] = jnp.broadcast_to(ids_in[0:1, :], (L, R)).T
    lqcol[...] = jnp.broadcast_to(lq_in[0:1, :], (L, R)).T

    def forward(t, dest):
        for c in loads[t]:
            c.wait()
        o = t * WROWS
        xb[t] = xf[t].astype(BF16)
        for c in range(12):
            w1b[t, :, L * c:L * c + L] = S[o + D * c:o + D * (c + 1), :].astype(BF16)
        for c in range(3):
            w2b[t, :, L * c:L * c + L] = S[o + 4608 + H * c:o + 4608 + H * (c + 1), :].astype(BF16)
        for c in range(3):
            w3b[t, :, L * c:L * c + L] = S[o + 9216 + D * c:o + 9216 + D * (c + 1), :].astype(BF16)

        def first(n, _):
            cols = pl.ds(pl.multiple_of(n * 256, 256), 256)
            h1[t, :, cols] = jnp.maximum(dot(xb[t], w1b[t, :, cols]), 0.0).astype(BF16)
            return 0
        lax.fori_loop(0, 6, first, 0)
        h2[t] = jnp.maximum(dot(h1[t], w2b[t]), 0.0).astype(BF16)
        z = dot(h2[t], w3b[t])
        inv = lax.rsqrt(jnp.sum(z * z, axis=1, keepdims=True) + EPS)
        inv_ref[t] = jnp.broadcast_to(inv, (R, L))
        e = z * inv
        e_ref[t] = e
        dest[pl.ds(pl.multiple_of(me * R, R), R), :] = e.astype(BF16)

    class Gather:
        def __init__(self, base, part, full):
            self.base, self.part, self.full = base, part, full

        def _send(self, j, pos, rel):
            for p in range(3):
                o = [DIMS[(p + i) % 3] for i in range(3)]
                m = sum(o[i] for i in rel)
                r = self.part(p, chips[m])
                send(r, r, self.base + 7 * p + j, nbr(o[pos]))

        def _wait(self, j, rel):
            for p in range(3):
                o = [DIMS[(p + i) % 3] for i in range(3)]
                m = sum(o[i] for i in rel)
                arrived(self.part(p, chips[m]), self.base + 7 * p + j)

        def _cross(self, m):
            r = self.full(chips[m], core)
            send(r, r, self.base + 21 + m, partner)

        def start(self):
            self._send(0, 0, ())
            self._send(1, 1, ())
            self._send(3, 2, ())
            self._cross(0)

        def f1(self):
            self._wait(0, (0,))
            self._send(2, 1, (0,))
            self._send(4, 2, (0,))

        def f2(self):
            self._wait(1, (1,))
            self._send(5, 2, (1,))

        def f2b(self):
            self._wait(3, (2,))
            for m in (4, 2, 1):
                self._cross(m)

        def f3(self):
            self._wait(2, (0, 1))
            self._send(6, 2, (0, 1))

        def f4(self):
            self._wait(4, (0, 2))
            self._wait(5, (1, 2))
            for m in (6, 5, 3):
                self._cross(m)

        def f5(self):
            self._wait(6, (0, 1, 2))
            self._cross(7)

        def other(self, *ms):
            for m in ms:
                arrived(self.full(chips[m], 1 - core), self.base + 21 + m)

    def emb_gather(buf, base):
        def rows(c, k):
            return pl.ds(pl.multiple_of((c * 2 + k) * R, R), R)
        return Gather(base, lambda p, c: buf.at[rows(c, core), pl.ds(L * p, L)],
                      lambda c, k: buf.at[rows(c, k), :])

    gv = emb_gather(v_all, V_AG)
    gu = emb_gather(u_all, U_AG)

    def wrow(t, p, r):
        return t * WROWS + p * PACK + r

    def wblk(t, p, c, k):
        return pl.ds(pl.multiple_of(wrow(t, p, 0) + (k * 8 + c) * BLK, 8), BLK)

    def add_into(dst_rows, src):
        S[dst_rows, :] += src

    class Reduce:
        def __init__(self, t):
            self.t, self.base = t, AR[t]

        def cross(self):
            for p in range(3):
                rows = pl.ds(pl.multiple_of(wrow(self.t, p, 0) + (1 - core) * HALF, 8), HALF)
                send(S.at[rows, :], recv_d.at[self.t, p], self.base + p, partner)

        def _orders(self):
            for p in range(3):
                yield p, [DIMS[(p + i) % 3] for i in range(3)]

        def p1(self):
            t = self.t
            for p in range(3):
                arrived(recv_d.at[t, p], self.base + p)
            for p in range(3):
                for q in range(8):
                    rows = pl.ds(pl.multiple_of(wrow(t, p, 0) + core * HALF + q * BLK, 8), BLK)
                    S[rows, :] += recv_d[t, p, q * BLK:(q + 1) * BLK, :]
            for s in range(4):
                for p, (a, b, c) in self._orders():
                    m = (b + c, b, c, 0)[s]
                    send(S.at[wblk(t, p, chips[a ^ m], core), :], rb1.at[t, p, s],
                         self.base + 3 + 7 * p + s, nbr(a))

        def p2(self):
            t = self.t
            for s in range(2):
                for p, (a, b, c) in self._orders():
                    m = (b + c, b)[s]
                    arrived(rb1.at[t, p, s], self.base + 3 + 7 * p + s)
                    add_into(wblk(t, p, chips[m], core), rb1[t, p, s])
                    send(S.at[wblk(t, p, chips[m], core), :], rb2.at[t, p, s],
                         self.base + 3 + 7 * p + 4 + s, nbr(b))

        def p2b(self):
            t = self.t
            for s in (2, 3):
                for p, (a, b, c) in self._orders():
                    m = (b + c, b, c, 0)[s]
                    arrived(rb1.at[t, p, s], self.base + 3 + 7 * p + s)
                    add_into(wblk(t, p, chips[m], core), rb1[t, p, s])

        def p3(self):
            t = self.t
            for p, (a, b, c) in self._orders():
                arrived(rb2.at[t, p, 0], self.base + 3 + 7 * p + 4)
                add_into(wblk(t, p, chips[c], core), rb2[t, p, 0])
                send(S.at[wblk(t, p, chips[c], core), :], rb3.at[t, p],
                     self.base + 3 + 7 * p + 6, nbr(c))
            for p, (a, b, c) in self._orders():
                arrived(rb2.at[t, p, 1], self.base + 3 + 7 * p + 5)
                add_into(wblk(t, p, chips[0], core), rb2[t, p, 1])

        def p4(self):
            t = self.t
            for p, (a, b, c) in self._orders():
                arrived(rb3.at[t, p], self.base + 3 + 7 * p + 6)
                S[wblk(t + 1, p, chips[0], core), :] = S[wblk(t, p, chips[0], core), :] + rb3[t, p]

    class GradGather(Gather):
        def __init__(self, t):
            super().__init__(AR[t] + 24, lambda p, c: S.at[wblk(t + 1, p, c, core), :], None)
            self.t = t

        def _cross(self, m):
            for p in range(3):
                r = S.at[wblk(self.t + 1, p, chips[m], core), :]
                send(r, r, N_SEM + self.t * 24 + m * 3 + p, partner)

        def other(self, *ms):
            for m in ms:
                for p in range(3):
                    arrived(S.at[wblk(self.t + 1, p, chips[m], 1 - core), :], N_SEM + self.t * 24 + m * 3 + p)

    def push_all(buf, base):
        for i in range(1, NDEV):
            send(buf.at[me], buf.at[me], base + i, lax.rem(me + i, NDEV))

    def pull_all(buf, base):
        for i in range(1, NDEV):
            arrived(buf.at[lax.rem(me + NDEV - i, NDEV)], base + i)

    def order(i):
        return 4 - 2 * i + lax.div(i * (i - 1), 2)

    def device_of(slot):
        g = lax.div(slot + 1, 3)
        i = lax.rem(slot + 1, 3)
        near = order(i)
        m = jnp.where(slot < 2, 0, jnp.where(g < 3, near, jnp.where(g < 5, 7 - near, 7)))
        oth = jnp.where(slot < 2, slot, jnp.where(slot < 14, lax.rem(g - 1, 2), slot - 14))
        k = core + oth - 2 * core * oth
        return flip(m) * 2 + k

    def rowsl(q):
        return pl.ds(pl.multiple_of(q * R, R), R)

    def diag(r0, t):
        return (lax.broadcasted_iota(jnp.int32, (CH, L), 0) + r0
                == lax.broadcasted_iota(jnp.int32, (CH, L), 1) + L * t)

    def row_slot(slot, own):
        q = me if own else device_of(slot)
        s512 = dot(u_all[rowsl(me), :], v_all[rowsl(q), :], NT)
        for t in range(4):
            S[pl.ds(pl.multiple_of((slot * 4 + t) * R, R), R), :] = s512[:, L * t:L * t + L]

        def chunk(r, _):
            r0 = pl.multiple_of(r * CH, CH)
            rs = pl.ds(r0, CH)
            idc = idcol[rs, :]
            mo = m_ref[rs, :]
            vals = []
            pos = jnp.zeros((CH, L), F32)
            for t in range(4):
                off = pl.ds(pl.multiple_of((slot * 4 + t) * R + r0, CH), CH)
                s = S[off, :] * SCALE - lq_all[q, 0:1, L * t:L * t + L]
                hit = idc == ids_all[q, 0:1, L * t:L * t + L]
                if own:
                    dg = diag(r0, t)
                    pos = pos + jnp.where(dg, s, 0.0)
                    hit = jnp.logical_and(hit, jnp.logical_not(dg))
                s = jnp.where(hit, -jnp.inf, s)
                S[off, :] = s
                vals.append(s)
            if own:
                pos_ref[rs, :] = pos
            mn = jnp.maximum(jnp.maximum(mo, jnp.maximum(vals[0], vals[1])), jnp.maximum(vals[2], vals[3]))
            tot = l_ref[rs, :] * jnp.exp(mo - mn)
            for s in vals:
                tot = tot + jnp.exp(s - mn)
            l_ref[rs, :] = tot
            m_ref[rs, :] = mn
            return 0
        lax.fori_loop(0, R // CH, chunk, 0)

    def row_slots(a, b):
        lax.fori_loop(a, b, lambda s, c: (row_slot(s, False), c)[1], 0)

    def row_finish():
        m = m_ref[...]
        top = jnp.max(m, axis=1, keepdims=True)
        tot = jnp.sum(l_ref[...] * jnp.exp(m - top), axis=1, keepdims=True)
        inv = 1.0 / (tot * float(B))
        cost = top + jnp.log(tot) - jnp.sum(pos_ref[...], axis=1, keepdims=True)
        m_ref[...] = jnp.broadcast_to(top, (R, L))
        l_ref[...] = jnp.broadcast_to(inv, (R, L))
        lane = lax.broadcasted_iota(jnp.int32, (R, L), 1)
        pack = jnp.where(lane == 0, top, jnp.where(lane == 1, inv, jnp.where(lane == 2, cost, 0.0)))
        st_all[me] = pack.T[0:8, :]

    def du_slot(slot, own):
        q = me if own else device_of(slot)

        def chunk(r, _):
            r0 = pl.multiple_of(r * CH, CH)
            rs = pl.ds(r0, CH)
            mc = m_ref[rs, :]
            ic = l_ref[rs, :]
            for t in range(4):
                off = pl.ds(pl.multiple_of((slot * 4 + t) * R + r0, CH), CH)
                g = jnp.exp(S[off, :] - mc) * ic
                if own:
                    g = g - jnp.where(diag(r0, t), 1.0 / B, 0.0)
                G[rs, L * t:L * t + L] = g.astype(BF16)
            return 0
        lax.fori_loop(0, R // CH, chunk, 0)
        part = dot(G[...], v_all[rowsl(q), :])
        acc[...] = part if own else acc[...] + part

    def du_slots(a, b):
        lax.fori_loop(a, b, lambda s, c: (du_slot(s, False), c)[1], 0)

    def dv_slot(slot, own):
        q = me if own else device_of(slot)
        big[...] = dot(v_all[rowsl(me), :], u_all[rowsl(q), :], NT)

        def chunk(r, _):
            r0 = pl.multiple_of(r * CH, CH)
            rs = pl.ds(r0, CH)
            idc = idcol[rs, :]
            lqc = lqcol[rs, :]
            for t in range(4):
                cs = slice(L * t, L * t + L)
                s = big[rs, cs] * SCALE - lqc
                hit = idc == ids_all[q, 0:1, cs]
                if own:
                    dg = diag(r0, t)
                    hit = jnp.logical_and(hit, jnp.logical_not(dg))
                g = jnp.exp(jnp.where(hit, -jnp.inf, s) - st_all[q, 0:1, cs]) * st_all[q, 1:2, cs]
                if own:
                    g = g - jnp.where(dg, 1.0 / B, 0.0)
                G[rs, cs] = g.astype(BF16)
            return 0
        lax.fori_loop(0, R // CH, chunk, 0)
        part = dot(G[...], u_all[rowsl(q), :])
        acc[...] = part if own else acc[...] + part

    def dv_slots(a, b):
        lax.fori_loop(a, b, lambda s, c: (dv_slot(s, False), c)[1], 0)

    def put(t, r0, val):
        n = val.shape[0]
        for p in range(3):
            S[pl.ds(pl.multiple_of(wrow(t, p, 0) + r0, 8), n), :] = val[:, L * p:L * p + L]

    def backward(t):
        d = acc[...] * SCALE
        e = e_ref[t]
        inv = inv_ref[t]
        s = jnp.sum(e * d, axis=1, keepdims=True)
        dzb = ((d - e * s) * jnp.concatenate([inv, inv, inv], axis=1)).astype(BF16)
        put(t, H, dot(h2[t], dzb, TN))
        da2 = jnp.where(h2[t] > 0, dot(dzb, w3b[t], NT), 0.0).astype(BF16)
        G[:, 0:D] = da2

        def mid(c, _):
            cols = pl.ds(pl.multiple_of(c * D, L), D)
            g2 = G[:, 0:D]
            put(t, c * D, dot(h1[t, :, cols], g2, TN))
            g1 = dot(g2, w2b[t, cols, :], NT)
            da1[...] = jnp.where(h1[t, :, cols] > 0, g1, 0.0).astype(BF16)
            put(t, H + D + c * D, dot(xb[t], da1[...], TN))
            return 0
        lax.fori_loop(0, 4, mid, 0)

    outs = {0: (gi1, gi2, gi3), 1: (gu1, gu2, gu3)}
    writes = []

    def write_out(t):
        g1, g2, g3 = outs[t]
        k = 0
        for p in range(3):
            pc = pl.ds(L * p, L)
            jobs = [(wrow(t + 1, p, 0), H, g2.at[:, pc]), (wrow(t + 1, p, H), D, g3.at[:, pc])]
            jobs += [(wrow(t + 1, p, H + D + D * c), D, g1.at[:, pl.ds(D * c + L * p, L)]) for c in range(4)]
            for r0, n, dst in jobs:
                c = pltpu.make_async_copy(S.at[pl.ds(r0, n), :], dst, out_sem.at[t, k])
                c.start()
                writes.append(c)
                k += 1

    forward(0, v_all)
    pl.semaphore_wait(barrier, NDEV - 1)
    gv.start()
    push_all(ids_all, IDS)
    push_all(lq_all, LQS)
    forward(1, u_all)
    gv.f1()
    m_ref[...] = jnp.full((R, L), LOWEST, F32)
    l_ref[...] = jnp.zeros((R, L), F32)
    row_slot(0, True)
    pull_all(ids_all, IDS)
    pull_all(lq_all, LQS)
    gv.other(0)
    gv.f2()
    row_slots(1, 2)
    gv.f2b()
    row_slots(2, 5)
    gv.f3()
    gu.start()
    gv.other(4, 2, 1)
    row_slots(5, 8)
    gv.f4()
    row_slots(8, 11)
    gv.f5()
    gv.other(6, 5, 3)
    row_slots(11, 15)
    gv.other(7)
    row_slots(15, 16)
    row_finish()
    push_all(st_all, STS)
    gu.f1()
    gu.f2()
    du_slot(0, True)
    du_slots(1, 4)
    gu.f2b()
    gu.f3()
    du_slots(4, 12)
    gu.f4()
    du_slots(12, 16)
    gu.f5()
    backward(1)
    ru, ri = Reduce(1), Reduce(0)
    au, ai = GradGather(1), GradGather(0)
    ru.cross()
    pull_all(st_all, STS)
    gu.other(0, 1, 2, 3, 4, 5, 6, 7)
    dv_slot(0, True)
    dv_slots(1, 3)
    ru.p1()
    dv_slots(3, 7)
    ru.p2()
    dv_slots(7, 11)
    ru.p2b()
    dv_slots(11, 14)
    ru.p3()
    dv_slots(14, 16)
    backward(0)
    ru.p4()
    flush()
    au.start()
    ri.cross()
    au.f1()
    au.f2()
    ri.p1()
    au.f2b()
    au.f3()
    au.f4()
    au.f5()
    ri.p2()
    ri.p2b()
    au.other(0, 1, 2, 3, 4, 5, 6, 7)
    write_out(1)
    ri.p3()
    ri.p4()
    ai.start()
    total = jnp.sum(jnp.sum(st_all[...], axis=0)[2:3, :]) * (1.0 / B)
    loss[...] = jnp.full((8, L), total, F32)
    ai.f1()
    ai.f2()
    ai.f2b()
    ai.f3()
    ai.f4()
    ai.f5()
    ai.other(0, 1, 2, 3, 4, 5, 6, 7)
    write_out(0)
    flush()
    for c in writes:
        c.wait()


def solution(mesh):
    vm = pl.BlockSpec(memory_space=pltpu.VMEM)
    hbm = pl.BlockSpec(memory_space=pl.ANY)
    shp = jax.ShapeDtypeStruct
    n_sem = N_SEM + 48

    def device_step(user_x, item_x, item_id, log_q, user_w1, user_w2, user_w3, item_w1, item_w2, item_w3):
        ids8 = jnp.broadcast_to(item_id[None, :], (8, R))
        lq8 = jnp.broadcast_to(log_q[None, :], (8, R))
        V = pltpu.VMEM
        out = pl.pallas_call(
            kernel,
            out_shape=(shp((8, L), F32), shp((D, H), F32), shp((H, D), F32), shp((D, D), F32),
                       shp((D, H), F32), shp((H, D), F32), shp((D, D), F32)),
            in_specs=[hbm, hbm, vm, vm] + [hbm] * 6,
            out_specs=(vm,) + (hbm,) * 6,
            scratch_shapes=[
                V((64 * R, L), F32), V((B, D), BF16), V((B, D), BF16),
                V((2, R, D), F32), V((2, R, D), BF16), V((2, R, H), BF16), V((2, R, D), BF16),
                V((2, R, D), F32), V((2, R, L), F32),
                V((2, D, H), BF16), V((2, H, D), BF16), V((2, D, D), BF16), V((R, D), BF16),
                V((NDEV, 8, R), jnp.int32), V((NDEV, 8, R), F32), V((NDEV, 8, R), F32),
                V((R, L), jnp.int32), V((R, L), F32), V((R, L), F32), V((R, L), F32), V((R, L), F32),
                V((R, R), BF16), V((R, D), F32), V((R, R), F32),
                V((2, 3, HALF, L), F32), V((2, 3, 4, BLK, L), F32), V((2, 3, 2, BLK, L), F32),
                V((2, 3, BLK, L), F32),
                pltpu.SemaphoreType.DMA((n_sem,)), pltpu.SemaphoreType.DMA((n_sem,)),
                pltpu.SemaphoreType.DMA((2, 19)), pltpu.SemaphoreType.DMA((2, 18)),
            ],
            compiler_params=pltpu.CompilerParams(collective_id=0, has_side_effects=True,
                                                 vmem_limit_bytes=67043328),
            name='step',
        )(user_x, item_x, ids8, lq8, user_w1, user_w2, user_w3, item_w1, item_w2, item_w3)
        return (out[0][0, 0],) + tuple(out[1:])

    batch_spec = P('dp', None)
    vec_spec = P('dp')
    whole = P()
    return jax.shard_map(device_step, mesh=mesh,
                         in_specs=(batch_spec, batch_spec, vec_spec, vec_spec, whole, whole, whole, whole, whole, whole),
                         out_specs=(whole,) * 7, check_vma=False)
```

time: 368 us -> 175 us (0.48)
  waiting for transfers between devices: 191 us -> 0 us
  Pallas kernels: 0 us -> 158 us
  blocking collectives: 59.9 us -> 0 us
  matrix products: 57.7 us -> 0 us
  other arithmetic: 22.4 us -> 0 us
  between operations: 15.8 us -> 0.65 us
  local copies, waits for them, and re-layouts: 20.6 us -> 14.9 us
    pallas_call x0 -> x1, Pallas kernels: none -> 158 us  [device_step(): pl.pallas_call(kernel, out_shape=(shp((8, L), F32), shp((D, H), F32), shp...]
    psum x1 -> x0, waiting for transfers between devices: 98.9 us -> none  [device_step(): lax.psum((jnp.sum(log_norm - pos_score),) + user_grads + item_grads, 'dp')]
    reduce_scatter x1 -> x0, waiting for transfers between devices: 70.6 us -> none  [device_step(): lax.psum_scatter(item_part, 'dp', scatter_dimension=0, tiled=True)]
    dot_general x17 -> x0, matrix products: 57.7 us -> none  [the longest x1 16.3 us: device_step(): lax.dot_general(user_half, item_all, COL_DIMS, preferred_element_type=jnp...]
    psum x1 -> x0, blocking collectives: 32.7 us -> none  [device_step(): lax.psum((jnp.sum(log_norm - pos_score),) + user_grads + item_grads, 'dp')]
    all_gather x2 -> x0, blocking collectives: 27.2 us -> none  [the longest x1 15.2 us: device_step(): logq_all = lax.all_gather(log_q, 'dp', axis=0, tiled=True)]
    all_gather x1 -> x0, waiting for transfers between devices: 21.2 us -> none  [device_step(): item_all = lax.all_gather(item_half, 'dp', axis=0, tiled=True)]
    reduce_sum x4 -> x0, other arithmetic: 11.9 us -> none  [the longest x1 8.12 us: device_step(): row_total = jnp.sum(exp_scores, axis=1, keepdims=True)]
  transfers between devices with their start and end apart: 3 -> 0, of which waited for: 3 -> 0; matrix products, arithmetic and copies ran while one was open for 5% -> 0% of each run, Pallas kernels for 0% -> 0%
where the time goes in v1:
time: 175 us; the launch traced here: 173 us
  Pallas kernels  158 us (90%)
  local copies, waits for them, and re-layouts  14.9 us (9%)
    pallas_call x1, Pallas kernels, device_step(): pl.pallas_call(kernel, out_shape=(shp((8, L), F32), shp((D, H), F32), shp...  158 us
    unnamed x16, local copies, waits for them, and re-layouts  11.1 us

profile of v1, /device:TPU:0, one launch (start us, length us, event | category | flops | bytes accessed | tf_op | source)
XLA Modules:
  0.0 173.3 jit_solution(7188482753180706389)
XLA Ops:
  0.6 1.3 broadcast_in_dim.4.ids_in
  1.9 1.3 broadcast_in_dim.5.lq_in
  3.2 157.8 %step.1 = (f32[8,128]{1,0:T(8,128)}, f32[384,1536]{1,0:T(8,128)}, f32[1536,384]{1,0:T(8,128)}, f32[384,384]{1,0:T(8,128)}, f32[384,1536]{1,0:T(8,128)}, /*index=5*/f32[1536,384]{1,0:T(8,128)}, f32[384,384]{1,0:T(8,128)}) custom-call(f32[512,384]{1,0:T(8,128)} %ux.1, f32[512,384]{1,0:T(8,128)} %ix.1, s32[8,512]{1,0:T(8,128)} %broadcast_in_dim.4.ids_in, ...), custom_call_target="tpu_custom_call" | custom-call | tf_op jit(solution)/shard_map/step/pallas_call | solution.py:555
  161.0 1.2 slice.3
  162.2 0.0 copy-start.2
  162.2 3.4 %copy.23 = f32[384,1536]{1,0:T(8,128)} copy(f32[384,1536]{1,0:T(8,128)} %get-tuple-element.29) | data formatting | bytes 4718592
  165.6 0.0 copy-done.2
  165.6 0.0 copy-start.4
  165.6 0.0 copy-start.1
  165.6 1.4 copy.24
  167.0 0.0 copy-done.4
  167.0 0.8 copy.25
  167.8 0.7 copy-done.1
  168.5 0.0 copy-start
  168.5 1.4 copy.26
  169.9 1.1 copy-done
  171.0 0.0 copy-start.3
  171.0 1.4 copy.27
  172.4 0.1 copy-done.3
  172.5 0.8 copy.28
Async XLA Ops:
  162.2 3.4 %copy-start.2 = (f32[1536,384]{1,0:T(8,128)S(1)}, f32[1536,384]{1,0:T(8,128)}, u32[]{:S(2)}) copy-start(f32[1536,384]{1,0:T(8,128)} %get-tuple-element.30) | copy-start | bytes 7077892
  165.6 1.4 copy-start.4
  165.6 2.9 %copy-start.1 = (f32[384,1536]{1,0:T(8,128)S(1)}, f32[384,1536]{1,0:T(8,128)}, u32[]{:S(2)}) copy-start(f32[384,1536]{1,0:T(8,128)} %get-tuple-element.32) | copy-start | bytes 7077892
  168.5 2.5 %copy-start = (f32[1536,384]{1,0:T(8,128)S(1)}, f32[1536,384]{1,0:T(8,128)}, u32[]{:S(2)}) copy-start(f32[1536,384]{1,0:T(8,128)} %get-tuple-element.33) | copy-start | bytes 7077892
  171.0 1.5 copy-start.3

commit v2 on v1

--- a/solution.py
+++ b/solution.py
@@ -15,9 +15,11 @@
 BLK = 216
 HALF = 8 * BLK
 PACK = 2 * HALF
+SEG = 960
 WROWS = 3 * PACK
 L = 128
 CH = 64
+VMEM_LIMIT = 56000000
 F32, BF16 = jnp.float32, jnp.bfloat16
 MESH = pl.DeviceIdType.MESH
 NT = (((1,), (1,)), ((), ()))
@@ -25,8 +27,8 @@
 LOWEST = float(jnp.finfo(jnp.float32).min)
 V_AG, U_AG = 0, 29
 IDS, LQS, STS = 58, 74, 90
-AR = (106, 162)
-N_SEM = 218
+AR = (106, 154)
+N_SEM = 202
 DIMS = (4, 2, 1)
 
 
@@ -35,10 +37,10 @@
 
 
 def kernel(ux, ix, ids_in, lq_in, uw1, uw2, uw3, iw1, iw2, iw3,
-           loss, gu1, gu2, gu3, gi1, gi2, gi3,
-           S, v_all, u_all, xf, xb, h1, h2, e_ref, inv_ref, w1b, w2b, w3b, da1,
+           loss, grads,
+           S, v_all, u_all, xb, h1, h2, e_ref, inv_ref, w1b, w2b, w3b, da1,
            ids_all, lq_all, st_all, idcol, lqcol, m_ref, l_ref, pos_ref, G, acc, big,
-           recv_d, rb1, rb2, rb3, send_sem, recv_sem, loc_sem, out_sem):
+           recv_d, rb1, rb2, rb3, send_sem, recv_sem, loc_sem, ack):
     me = lax.axis_index('dp')
     core = lax.rem(me, 2)
     chip = lax.div(me, 2)
@@ -92,7 +94,8 @@
 
     for t, (xr, w1, w2, w3) in enumerate(((ix, iw1, iw2, iw3), (ux, uw1, uw2, uw3))):
         o = t * WROWS
-        load(t, xr, xf.at[t], 0)
+        for c in range(3):
+            load(t, xr.at[:, pl.ds(L * c, L)], S.at[pl.ds(2 * WROWS + (3 * t + c) * R, R), :], 19 + c)
         for c in range(12):
             load(t, w1.at[:, pl.ds(L * c, L)], S.at[pl.ds(o + D * c, D), :], 1 + c)
         for c in range(3):
@@ -102,14 +105,16 @@
 
     ids_all[me] = ids_in[...]
     lq_all[me] = lq_in[...]
-    idcol[...] = jnp.broadcast_to(ids_in[0:1, :], (L, R)).T
-    lqcol[...] = jnp.broadcast_to(lq_in[0:1, :], (L, R)).T
+    for t in range(4):
+        idcol[L * t:L * t + L, :] = jnp.broadcast_to(ids_in[t:t + 1, :], (L, L)).T
+        lqcol[L * t:L * t + L, :] = jnp.broadcast_to(lq_in[t:t + 1, :], (L, L)).T
 
     def forward(t, dest):
         for c in loads[t]:
             c.wait()
         o = t * WROWS
-        xb[t] = xf[t].astype(BF16)
+        for c in range(3):
+            xb[t, :, L * c:L * c + L] = S[2 * WROWS + (3 * t + c) * R:2 * WROWS + (3 * t + c + 1) * R, :].astype(BF16)
         for c in range(12):
             w1b[t, :, L * c:L * c + L] = S[o + D * c:o + D * (c + 1), :].astype(BF16)
         for c in range(3):
@@ -211,10 +216,15 @@
         def __init__(self, t):
             self.t, self.base = t, AR[t]
 
-        def cross(self):
+        def _segment(self, i):
+            o, n = ((0, SEG), (SEG, HALF - SEG))[i]
             for p in range(3):
-                rows = pl.ds(pl.multiple_of(wrow(self.t, p, 0) + (1 - core) * HALF, 8), HALF)
-                send(S.at[rows, :], recv_d.at[self.t, p], self.base + p, partner)
+                rows = pl.ds(pl.multiple_of(wrow(self.t, p, 0) + (1 - core) * HALF + o, 8), n)
+                yield S.at[rows, :], recv_d.at[p, pl.ds(o, n), :], self.base + 2 * p + i
+
+        def cross(self, i):
+            for src, dst, k in self._segment(i):
+                send(src, dst, k, partner)
 
         def _orders(self):
             for p in range(3):
@@ -222,67 +232,70 @@
 
         def p1(self):
             t = self.t
-            for p in range(3):
-                arrived(recv_d.at[t, p], self.base + p)
+            for i in range(2):
+                for src, dst, k in self._segment(i):
+                    arrived(dst, k)
             for p in range(3):
                 for q in range(8):
                     rows = pl.ds(pl.multiple_of(wrow(t, p, 0) + core * HALF + q * BLK, 8), BLK)
-                    S[rows, :] += recv_d[t, p, q * BLK:(q + 1) * BLK, :]
+                    S[rows, :] += recv_d[p, q * BLK:(q + 1) * BLK, :]
+            if t == 1:
+                pl.semaphore_signal(ack, inc=1, device_id=(partner,), device_id_type=MESH)
             for s in range(4):
                 for p, (a, b, c) in self._orders():
                     m = (b + c, b, c, 0)[s]
-                    send(S.at[wblk(t, p, chips[a ^ m], core), :], rb1.at[t, p, s],
-                         self.base + 3 + 7 * p + s, nbr(a))
+                    send(S.at[wblk(t, p, chips[a ^ m], core), :], rb1.at[p, s],
+                         self.base + 6 + 7 * p + s, nbr(a))
 
         def p2(self):
             t = self.t
             for s in range(2):
                 for p, (a, b, c) in self._orders():
                     m = (b + c, b)[s]
-                    arrived(rb1.at[t, p, s], self.base + 3 + 7 * p + s)
-                    add_into(wblk(t, p, chips[m], core), rb1[t, p, s])
-                    send(S.at[wblk(t, p, chips[m], core), :], rb2.at[t, p, s],
-                         self.base + 3 + 7 * p + 4 + s, nbr(b))
+                    arrived(rb1.at[p, s], self.base + 6 + 7 * p + s)
+                    add_into(wblk(t, p, chips[m], core), rb1[p, s])
+                    send(S.at[wblk(t, p, chips[m], core), :], rb2.at[p, s],
+                         self.base + 6 + 7 * p + 4 + s, nbr(b))
 
         def p2b(self):
             t = self.t
             for s in (2, 3):
                 for p, (a, b, c) in self._orders():
                     m = (b + c, b, c, 0)[s]
-                    arrived(rb1.at[t, p, s], self.base + 3 + 7 * p + s)
-                    add_into(wblk(t, p, chips[m], core), rb1[t, p, s])
+                    arrived(rb1.at[p, s], self.base + 6 + 7 * p + s)
+                    add_into(wblk(t, p, chips[m], core), rb1[p, s])
 
         def p3(self):
             t = self.t
             for p, (a, b, c) in self._orders():
-                arrived(rb2.at[t, p, 0], self.base + 3 + 7 * p + 4)
-                add_into(wblk(t, p, chips[c], core), rb2[t, p, 0])
-                send(S.at[wblk(t, p, chips[c], core), :], rb3.at[t, p],
-                     self.base + 3 + 7 * p + 6, nbr(c))
+                arrived(rb2.at[p, 0], self.base + 6 + 7 * p + 4)
+                add_into(wblk(t, p, chips[c], core), rb2[p, 0])
+                send(S.at[wblk(t, p, chips[c], core), :], rb3.at[p],
+                     self.base + 6 + 7 * p + 6, nbr(c))
             for p, (a, b, c) in self._orders():
-                arrived(rb2.at[t, p, 1], self.base + 3 + 7 * p + 5)
-                add_into(wblk(t, p, chips[0], core), rb2[t, p, 1])
+                arrived(rb2.at[p, 1], self.base + 6 + 7 * p + 5)
+                add_into(wblk(t, p, chips[0], core), rb2[p, 1])
 
         def p4(self):
             t = self.t
             for p, (a, b, c) in self._orders():
-                arrived(rb3.at[t, p], self.base + 3 + 7 * p + 6)
-                S[wblk(t + 1, p, chips[0], core), :] = S[wblk(t, p, chips[0], core), :] + rb3[t, p]
+                arrived(rb3.at[p], self.base + 6 + 7 * p + 6)
+                grads[wblk(t, p, chips[0], core), :] = S[wblk(t, p, chips[0], core), :] + rb3[p]
 
     class GradGather(Gather):
         def __init__(self, t):
-            super().__init__(AR[t] + 24, lambda p, c: S.at[wblk(t + 1, p, c, core), :], None)
+            super().__init__(AR[t] + 27, lambda p, c: grads.at[wblk(t, p, c, core), :], None)
             self.t = t
 
         def _cross(self, m):
             for p in range(3):
-                r = S.at[wblk(self.t + 1, p, chips[m], core), :]
+                r = grads.at[wblk(self.t, p, chips[m], core), :]
                 send(r, r, N_SEM + self.t * 24 + m * 3 + p, partner)
 
         def other(self, *ms):
             for m in ms:
                 for p in range(3):
-                    arrived(S.at[wblk(self.t + 1, p, chips[m], 1 - core), :], N_SEM + self.t * 24 + m * 3 + p)
+                    arrived(grads.at[wblk(self.t, p, chips[m], 1 - core), :], N_SEM + self.t * 24 + m * 3 + p)
 
     def push_all(buf, base):
         for i in range(1, NDEV):
@@ -326,8 +339,8 @@
             pos = jnp.zeros((CH, L), F32)
             for t in range(4):
                 off = pl.ds(pl.multiple_of((slot * 4 + t) * R + r0, CH), CH)
-                s = S[off, :] * SCALE - lq_all[q, 0:1, L * t:L * t + L]
-                hit = idc == ids_all[q, 0:1, L * t:L * t + L]
+                s = S[off, :] * SCALE - lq_all[q, t:t + 1, :]
+                hit = idc == ids_all[q, t:t + 1, :]
                 if own:
                     dg = diag(r0, t)
                     pos = pos + jnp.where(dg, s, 0.0)
@@ -395,7 +408,7 @@
             for t in range(4):
                 cs = slice(L * t, L * t + L)
                 s = big[rs, cs] * SCALE - lqc
-                hit = idc == ids_all[q, 0:1, cs]
+                hit = idc == ids_all[q, t:t + 1, :]
                 if own:
                     dg = diag(r0, t)
                     hit = jnp.logical_and(hit, jnp.logical_not(dg))
@@ -416,41 +429,40 @@
         for p in range(3):
             S[pl.ds(pl.multiple_of(wrow(t, p, 0) + r0, 8), n), :] = val[:, L * p:L * p + L]
 
-    def backward(t):
+    def backward(t, red, hooks):
         d = acc[...] * SCALE
         e = e_ref[t]
         inv = inv_ref[t]
         s = jnp.sum(e * d, axis=1, keepdims=True)
         dzb = ((d - e * s) * jnp.concatenate([inv, inv, inv], axis=1)).astype(BF16)
-        put(t, H, dot(h2[t], dzb, TN))
+        g3 = dot(h2[t], dzb, TN)
+        put(t, 2 * D, g3[:D // 2])
+        put(t, HALF + 2 * D, g3[D // 2:])
         da2 = jnp.where(h2[t] > 0, dot(dzb, w3b[t], NT), 0.0).astype(BF16)
         G[:, 0:D] = da2
 
-        def mid(c, _):
+        def mid(i):
+            c = lax.rem(i + 2 * (1 - core), 4)
+            base = lax.div(c, 2) * HALF + lax.rem(c, 2) * SEG
             cols = pl.ds(pl.multiple_of(c * D, L), D)
             g2 = G[:, 0:D]
-            put(t, c * D, dot(h1[t, :, cols], g2, TN))
+            put(t, base, dot(h1[t, :, cols], g2, TN))
             g1 = dot(g2, w2b[t, cols, :], NT)
             da1[...] = jnp.where(h1[t, :, cols] > 0, g1, 0.0).astype(BF16)
-            put(t, H + D + c * D, dot(xb[t], da1[...], TN))
-            return 0
-        lax.fori_loop(0, 4, mid, 0)
-
-    outs = {0: (gi1, gi2, gi3), 1: (gu1, gu2, gu3)}
-    writes = []
-
-    def write_out(t):
-        g1, g2, g3 = outs[t]
-        k = 0
-        for p in range(3):
-            pc = pl.ds(L * p, L)
-            jobs = [(wrow(t + 1, p, 0), H, g2.at[:, pc]), (wrow(t + 1, p, H), D, g3.at[:, pc])]
-            jobs += [(wrow(t + 1, p, H + D + D * c), D, g1.at[:, pl.ds(D * c + L * p, L)]) for c in range(4)]
-            for r0, n, dst in jobs:
-                c = pltpu.make_async_copy(S.at[pl.ds(r0, n), :], dst, out_sem.at[t, k])
-                c.start()
-                writes.append(c)
-                k += 1
+            put(t, base + D, dot(xb[t], da1[...], TN))
+
+        hooks[0]()
+        for i in range(2):
+            mid(i)
+            red.cross(i)
+        hooks[1]()
+        lax.fori_loop(2, 4, lambda i, x: (mid(i), x)[1], 0)
+
+    ru, ri = Reduce(1), Reduce(0)
+    au, ai = GradGather(1), GradGather(0)
+
+    def nothing():
+        pass
 
     forward(0, v_all)
     pl.semaphore_wait(barrier, NDEV - 1)
@@ -485,50 +497,48 @@
     gu.f1()
     gu.f2()
     du_slot(0, True)
-    du_slots(1, 4)
+    du_slots(1, 5)
     gu.f2b()
+    du_slots(5, 10)
     gu.f3()
-    du_slots(4, 12)
-    gu.f4()
-    du_slots(12, 16)
+    du_slots(10, 16)
+    backward(1, ru, (nothing, gu.f4))
     gu.f5()
-    backward(1)
-    ru, ri = Reduce(1), Reduce(0)
-    au, ai = GradGather(1), GradGather(0)
-    ru.cross()
     pull_all(st_all, STS)
-    gu.other(0, 1, 2, 3, 4, 5, 6, 7)
     dv_slot(0, True)
+    gu.other(0, 4, 2, 1, 6, 5, 3)
     dv_slots(1, 3)
     ru.p1()
+    gu.other(7)
     dv_slots(3, 7)
     ru.p2()
     dv_slots(7, 11)
     ru.p2b()
-    dv_slots(11, 14)
+    dv_slots(11, 13)
     ru.p3()
-    dv_slots(14, 16)
-    backward(0)
-    ru.p4()
-    flush()
-    au.start()
-    ri.cross()
+    dv_slots(13, 16)
+
+    def turn():
+        ru.p4()
+        au.start()
+        pl.semaphore_wait(ack, 1)
+
+    backward(0, ri, (turn, nothing))
     au.f1()
     au.f2()
     ri.p1()
     au.f2b()
     au.f3()
-    au.f4()
-    au.f5()
     ri.p2()
     ri.p2b()
-    au.other(0, 1, 2, 3, 4, 5, 6, 7)
-    write_out(1)
+    au.f4()
     ri.p3()
+    au.f5()
     ri.p4()
     ai.start()
+    au.other(0, 1, 2, 3, 4, 5, 6, 7)
     total = jnp.sum(jnp.sum(st_all[...], axis=0)[2:3, :]) * (1.0 / B)
-    loss[...] = jnp.full((8, L), total, F32)
+    loss[0, 0] = total
     ai.f1()
     ai.f2()
     ai.f2b()
@@ -536,46 +546,74 @@
     ai.f4()
     ai.f5()
     ai.other(0, 1, 2, 3, 4, 5, 6, 7)
-    write_out(0)
     flush()
-    for c in writes:
+
+
+def write_kernel(loss_in, grads, loss, gu1, gu2, gu3, gi1, gi2, gi3, sem):
+    loss[0, 0] = loss_in[0, 0]
+    copies = []
+    for t, (g1, g2, g3) in enumerate(((gi1, gi2, gi3), (gu1, gu2, gu3))):
+        for p in range(3):
+            pc = pl.ds(L * p, L)
+            for h in range(2):
+                o = t * WROWS + p * PACK + h * HALF
+                jobs = [(o + 2 * D, g3.at[pl.ds(h * (D // 2), D // 2), pc])]
+                for i in range(2):
+                    c = 2 * h + i
+                    jobs.append((o + i * SEG, g2.at[pl.ds(D * c, D), pc]))
+                    jobs.append((o + i * SEG + D, g1.at[:, pl.ds(D * c + L * p, L)]))
+                for r0, dst in jobs:
+                    src = grads.at[pl.ds(r0, dst.shape[0]), :]
+                    c = pltpu.make_async_copy(src, dst, sem.at[len(copies)])
+                    c.start()
+                    copies.append(c)
+    for c in copies:
         c.wait()
 
 
 def solution(mesh):
     vm = pl.BlockSpec(memory_space=pltpu.VMEM)
+    sm = pl.BlockSpec(memory_space=pltpu.SMEM)
     hbm = pl.BlockSpec(memory_space=pl.ANY)
     shp = jax.ShapeDtypeStruct
     n_sem = N_SEM + 48
 
     def device_step(user_x, item_x, item_id, log_q, user_w1, user_w2, user_w3, item_w1, item_w2, item_w3):
-        ids8 = jnp.broadcast_to(item_id[None, :], (8, R))
-        lq8 = jnp.broadcast_to(log_q[None, :], (8, R))
         V = pltpu.VMEM
-        out = pl.pallas_call(
+        loss, grads = pl.pallas_call(
             kernel,
-            out_shape=(shp((8, L), F32), shp((D, H), F32), shp((H, D), F32), shp((D, D), F32),
-                       shp((D, H), F32), shp((H, D), F32), shp((D, D), F32)),
+            out_shape=(shp((1, 1), F32), V((2 * WROWS, L), F32)),
             in_specs=[hbm, hbm, vm, vm] + [hbm] * 6,
-            out_specs=(vm,) + (hbm,) * 6,
+            out_specs=(sm, vm),
             scratch_shapes=[
                 V((64 * R, L), F32), V((B, D), BF16), V((B, D), BF16),
-                V((2, R, D), F32), V((2, R, D), BF16), V((2, R, H), BF16), V((2, R, D), BF16),
+                V((2, R, D), BF16), V((2, R, H), BF16), V((2, R, D), BF16),
                 V((2, R, D), F32), V((2, R, L), F32),
                 V((2, D, H), BF16), V((2, H, D), BF16), V((2, D, D), BF16), V((R, D), BF16),
-                V((NDEV, 8, R), jnp.int32), V((NDEV, 8, R), F32), V((NDEV, 8, R), F32),
+                V((NDEV, 4, L), jnp.int32), V((NDEV, 4, L), F32), V((NDEV, 8, R), F32),
                 V((R, L), jnp.int32), V((R, L), F32), V((R, L), F32), V((R, L), F32), V((R, L), F32),
                 V((R, R), BF16), V((R, D), F32), V((R, R), F32),
-                V((2, 3, HALF, L), F32), V((2, 3, 4, BLK, L), F32), V((2, 3, 2, BLK, L), F32),
-                V((2, 3, BLK, L), F32),
+                V((3, HALF, L), F32), V((3, 4, BLK, L), F32), V((3, 2, BLK, L), F32),
+                V((3, BLK, L), F32),
                 pltpu.SemaphoreType.DMA((n_sem,)), pltpu.SemaphoreType.DMA((n_sem,)),
-                pltpu.SemaphoreType.DMA((2, 19)), pltpu.SemaphoreType.DMA((2, 18)),
+                pltpu.SemaphoreType.DMA((2, 22)), pltpu.SemaphoreType.REGULAR,
             ],
             compiler_params=pltpu.CompilerParams(collective_id=0, has_side_effects=True,
-                                                 vmem_limit_bytes=67043328),
+                                                 vmem_limit_bytes=VMEM_LIMIT),
             name='step',
-        )(user_x, item_x, ids8, lq8, user_w1, user_w2, user_w3, item_w1, item_w2, item_w3)
-        return (out[0][0, 0],) + tuple(out[1:])
+        )(user_x, item_x, item_id.reshape(4, L), log_q.reshape(4, L),
+          user_w1, user_w2, user_w3, item_w1, item_w2, item_w3)
+        out = pl.pallas_call(
+            write_kernel,
+            out_shape=(shp((1, 1), F32), shp((D, H), F32), shp((H, D), F32), shp((D, D), F32),
+                       shp((D, H), F32), shp((H, D), F32), shp((D, D), F32)),
+            in_specs=[sm, vm],
+            out_specs=(sm,) + (hbm,) * 6,
+            scratch_shapes=[pltpu.SemaphoreType.DMA((60,))],
+            compiler_params=pltpu.CompilerParams(vmem_limit_bytes=1 << 20),
+            name='write',
+        )(loss, grads)
+        return (out[0].reshape(()),) + tuple(out[1:])
 
     batch_spec = P('dp', None)
     vec_spec = P('dp')

time: 175 us -> 149 us (0.85); the launches traced: 173 us -> 149 us
  local copies, waits for them, and re-layouts: 14.9 us -> 0 us
  Pallas kernels: 158 us -> 148 us
    unnamed x16 -> x0, local copies, waits for them, and re-layouts: 11.1 us -> none
    pallas_call x1 -> x2, Pallas kernels: 158 us -> 148 us  [the longest x1 143 us: device_step(): pl.pallas_call(kernel, out_shape=(shp((1, 1), F32), V((2 * WROWS, L), F32...]
    broadcast_in_dim x2 -> x0, local copies, waits for them, and re-layouts: 2.58 us -> none  [the longest x1 1.29 us: device_step(): ids8 = jnp.broadcast_to(item_id[None, :], (8, R))]
where the time goes in v2:
time: 149 us
  Pallas kernels  148 us (99%)
    pallas_call x1, Pallas kernels, device_step(): pl.pallas_call(kernel, out_shape=(shp((1, 1), F32), V((2 * WROWS, L), F32...  143 us
    pallas_call x1, Pallas kernels, device_step(): pl.pallas_call(write_kernel, out_shape=(shp((1, 1), F32), shp((D, H), F32...  5.6 us

profile of v2, /device:TPU:0, one launch (start us, length us, event | category | flops | bytes accessed | tf_op | source)
XLA Modules:
  0.0 149.3 jit_solution(11677144586723506701)
XLA Ops:
  0.6 142.9 %step.1 = (f32[1,1]{1,0:T(1,128)}, f32[20736,128]{1,0:T(8,128)S(1)}) custom-call(f32[512,384]{1,0:T(8,128)} %ux.1, f32[512,384]{1,0:T(8,128)} %ix.1, s32[4,128]{1,0:T(4,128)} %bitcast.3, f32[4,128]{1,0:T(4,128)} %bitcast.4, f32[384,1536]{1,0:T(8,128)} %uw1.1, f32[1536,384]{1,0:T(8,128)} %uw2.1, f32[384,384]{1,0:T(8,128)} %uw3.1, f32[384,1536]{1,0:T(8,128)} %iw1.1, ...), custom_call_target="tpu_custom_call" | custom-call | tf_op jit(solution)/shard_map/step/pallas_call | solution.py:583
  143.5 5.6 %write.1 = (f32[1,1]{1,0:T(1,128)}, f32[384,1536]{1,0:T(8,128)}, f32[1536,384]{1,0:T(8,128)}, f32[384,384]{1,0:T(8,128)}, f32[384,1536]{1,0:T(8,128)}, /*index=5*/f32[1536,384]{1,0:T(8,128)}, f32[384,384]{1,0:T(8,128)}) custom-call(f32[1,1]{1,0:T(1,128)} %get-tuple-element.16.loss_in, f32[20736,128]{1,0:T(8,128)S(1)} %get-tuple-element.17.grads), custom_call_target="tpu_custom_call" | custom-call | tf_op jit(solution)/shard_map/write/pallas_call | solution.py:606

commit v3 on v2

v3 whole, which is shorter than its diff:
```python
import jax
import jax.numpy as jnp
from jax import lax
from jax.experimental import pallas as pl
from jax.experimental.pallas import tpu as pltpu
from jax.sharding import PartitionSpec as P

SCALE = 20.0
EPS = 1e-6
NDEV = 16
R = 512
D = 384
H = 1536
B = R * NDEV
BLK = 216
HALF = 8 * BLK
N_SEND, N_RECV = 9, 89
PACK = 2 * HALF
SEG = 960
WROWS = 3 * PACK
L = 128
CH = 64
VMEM_LIMIT = 56000000
F32, BF16 = jnp.float32, jnp.bfloat16
MESH = pl.DeviceIdType.MESH
NT = (((1,), (1,)), ((), ()))
TN = (((0,), (0,)), ((), ()))
LOWEST = float(jnp.finfo(jnp.float32).min)
DIMS = (4, 2, 1)
CROSS = ((0,), (4, 2, 1), (6, 5, 3), (7,))


def dot(a, b, dims=(((1,), (0,)), ((), ()))):
    return lax.dot_general(a, b, dims, preferred_element_type=F32)


def kernel(ux, ix, ids_in, lq_in, uw1, uw2, uw3, iw1, iw2, iw3,
           loss, grads,
           S, v_all, u_all, xb, h1, h2, e_ref, inv_ref, w1b, w2b, w3b, da1,
           ids_all, lq_all, st_all, idcol, lqcol, m_ref, l_ref, pos_ref, G, acc, big,
           recv_d, rb1, rb2, rb3, send_sem, recv_sem, loc_sem, ack):
    made = [0, 0]

    def new_sems(kind, n):
        made[kind] += n
        return made[kind] - n

    me = lax.axis_index('dp')
    core = lax.rem(me, 2)
    chip = lax.div(me, 2)
    partner = me + 1 - 2 * core

    def flip(m):
        out = 0
        for d in DIMS:
            bit = lax.rem(lax.div(chip, d), 2)
            if isinstance(m, int):
                f = (m // d) % 2
            else:
                f = lax.rem(lax.div(m, d), 2)
            out = out + d * (bit + f - 2 * bit * f)
        return out

    chips = [flip(m) for m in range(8)]

    def nbr(d):
        return chips[d] * 2 + core

    def rc(src, dst, ssem, rsem, dev):
        return pltpu.make_async_remote_copy(src, dst, send_sem.at[ssem], recv_sem.at[rsem],
                                            device_id=(dev,), device_id_type=MESH)

    def send(src, dst, ssem, rsem, dev):
        rc(src, dst, ssem, rsem, dev).start()

    def arrived(ref, rsem):
        rc(ref, ref, 0, rsem, partner).wait_recv()

    def sent(ref, ssem):
        rc(ref, ref, ssem, 0, partner).wait_send()

    barrier = pltpu.get_barrier_semaphore()
    for i in range(1, NDEV):
        pl.semaphore_signal(barrier, inc=1, device_id=(lax.rem(me + i, NDEV),), device_id_type=MESH)

    def load(src, dst, t, k):
        pltpu.make_async_copy(src, dst, loc_sem.at[t, k]).start()

    def loaded(t, k, o, n):
        ref = S.at[pl.ds(o, n), :]
        pltpu.make_async_copy(ref, ref, loc_sem.at[t, k]).wait()

    W2_AT, W3_AT, STAGE = 12 * D, 12 * D + 3 * H, WROWS + 3 * R
    for t, (xr, w1, w2, w3) in enumerate(((ix, iw1, iw2, iw3), (ux, uw1, uw2, uw3))):
        o = t * STAGE

        def columns(src, at, rows, c, k):
            load(src.at[:, pl.ds(L * c, L)], S.at[pl.ds(o + at + rows * c, rows), :], t, k)
        for c in range(3):
            columns(xr, WROWS, R, c, 0)
        for c in range(12):
            columns(w1, 0, D, c, 1 + c // 4)
        for c in range(3):
            columns(w2, W2_AT, H, c, 4)
        for c in range(3):
            columns(w3, W3_AT, D, c, 5)

    ids_all[me] = ids_in[...]
    lq_all[me] = lq_in[...]
    for t in range(4):
        idcol[L * t:L * t + L, :] = jnp.broadcast_to(ids_in[t:t + 1, :], (L, L)).T
        lqcol[L * t:L * t + L, :] = jnp.broadcast_to(lq_in[t:t + 1, :], (L, L)).T

    def forward(t, dest):
        o = t * STAGE

        def take(dst, at, rows, c):
            dst[t, :, L * c:L * c + L] = S[o + at + rows * c:o + at + rows * (c + 1), :].astype(BF16)

        loaded(t, 0, o + WROWS, 3 * R)
        for c in range(3):
            take(xb, WROWS, R, c)
        for n in range(3):
            loaded(t, 1 + n, o + 4 * n * D, 4 * D)
            for c in range(4):
                take(w1b, 0, D, 4 * n + c)
            cols = slice(4 * n * L, 4 * (n + 1) * L)
            h1[t, :, cols] = jnp.maximum(dot(xb[t], w1b[t, :, cols]), 0.0).astype(BF16)
        loaded(t, 4, o + W2_AT, 3 * H)
        for c in range(3):
            take(w2b, W2_AT, H, c)
        h2[t] = jnp.maximum(dot(h1[t], w2b[t]), 0.0).astype(BF16)
        loaded(t, 5, o + W3_AT, 3 * D)
        for c in range(3):
            take(w3b, W3_AT, D, c)
        z = dot(h2[t], w3b[t])
        inv = lax.rsqrt(jnp.sum(z * z, axis=1, keepdims=True) + EPS)
        inv_ref[t] = jnp.broadcast_to(inv, (R, L))
        e = z * inv
        e_ref[t] = e
        dest[pl.ds(pl.multiple_of(me * R, R), R), :] = e.astype(BF16)

    class Gather:
        def __init__(self, part, full, units, ssem):
            self.part, self.full, self.units, self.ssem = part, full, units, ssem
            self.rsem = new_sems(1, 7)
            self.other_sem = None

        def _each(self, rel):
            for p in range(3):
                o = [DIMS[(p + i) % 3] for i in range(3)]
                yield p, o, self.part(p, chips[sum(o[i] for i in rel)])

        def _send(self, j, pos, rel):
            for p, o, r in self._each(rel):
                send(r, r, self.ssem, self.rsem + j, nbr(o[pos]))

        def _wait(self, j):
            arrived(self.units(3), self.rsem + j)

        def _cross(self, g):
            if self.other_sem is None:
                self.other_sem = self.cross_sems()
            for m in CROSS[g]:
                for r in self.full(chips[m]):
                    send(r, r, self.ssem, self.other_sem[g], partner)

        def start(self):
            self._send(0, 0, ())
            self._send(1, 1, ())
            self._send(3, 2, ())
            self._cross(0)

        def f1(self):
            self._wait(0)
            self._send(2, 1, (0,))
            self._send(4, 2, (0,))

        def f2(self):
            self._wait(1)
            self._send(5, 2, (1,))

        def f2b(self):
            self._wait(3)
            self._cross(1)

        def f3(self):
            self._wait(2)
            self._send(6, 2, (0, 1))

        def f4(self):
            self._wait(4)
            self._wait(5)
            self._cross(2)

        def f5(self):
            self._wait(6)
            self._cross(3)

    class Embeddings(Gather):
        def __init__(self, buf):
            def rows(c):
                return pl.ds(pl.multiple_of((c * 2 + core) * R, R), R)
            self.buf = buf
            super().__init__(lambda p, c: buf.at[rows(c), pl.ds(L * p, L)], lambda c: (buf.at[rows(c), :],),
                             lambda n: buf.at[pl.ds(0, n // 3 * R), :], new_sems(0, 1))

        def cross_sems(self):
            k = new_sems(1, 4)
            return range(k, k + 4)

        def other(self, g):
            arrived(self.units(3 * len(CROSS[g])), self.other_sem[g])

        def finish(self):
            sent(self.units(3 * (NDEV - 1)), self.ssem)

    gv = Embeddings(v_all)
    gu = Embeddings(u_all)

    def wrow(t, p, r):
        return t * WROWS + p * PACK + r

    class Reduce(Gather):
        def __init__(self, t, piece):
            self.t, self.piece = t, piece
            self.at, self.blk = ((0, SEG // 8), (SEG, (HALF - SEG) // 8))[piece]
            self.sub = (0, SEG // 8)[piece]
            super().__init__(lambda p, c: grads.at[self.rows(p, c), :], self._all_parts,
                             lambda n: grads.at[pl.ds(0, n * self.blk), :], new_sems(0, 1))
            self.red = new_sems(1, 8)

        def rows(self, p, c):
            return pl.ds(pl.multiple_of(wrow(self.t, p, 0) + core * HALF + self.at + c * self.blk, 8), self.blk)

        def _all_parts(self, c):
            return [grads.at[self.rows(p, c), :] for p in range(3)]

        def cross_sems(self):
            return (new_sems(1, 1),) * 4

        def other(self):
            arrived(self.units(24), self.other_sem[0])

        def finish(self):
            sent(self.units(90), self.ssem)

        def cross(self):
            n = 8 * self.blk
            for p in range(3):
                rows = pl.ds(pl.multiple_of(wrow(self.t, p, 0) + (1 - core) * HALF + self.at, 8), n)
                send(S.at[rows, :], recv_d.at[p, pl.ds(self.at, n), :], self.ssem, self.red, partner)

        def _orders(self):
            for p in range(3):
                yield p, [DIMS[(p + i) % 3] for i in range(3)]

        def _got(self, k):
            arrived(self.units(3), self.red + k)

        def _buf(self, ref, *i):
            return ref.at[(*i, pl.ds(self.sub, self.blk), slice(None))]

        def _add(self, p, c, ref, *i):
            rows = self.rows(p, c)
            S[rows, :] += self._buf(ref, *i)[...]

        def _pass(self, p, c, k, dev, ref, *i):
            send(S.at[self.rows(p, c), :], self._buf(ref, *i), self.ssem, self.red + k, nbr(dev))

        def p1(self):
            arrived(self.units(24), self.red)
            for p in range(3):
                for q in range(8):
                    rows = self.rows(p, q)
                    S[rows, :] += recv_d[p, self.at + q * self.blk:self.at + (q + 1) * self.blk, :]
            if self.t == 1:
                pl.semaphore_signal(ack.at[self.piece], inc=1, device_id=(partner,), device_id_type=MESH)
            for s in range(4):
                for p, (a, b, c) in self._orders():
                    self._pass(p, chips[a ^ (b + c, b, c, 0)[s]], 1 + s, a, rb1, p, s)

        def p2(self):
            for s in range(2):
                self._got(1 + s)
                for p, (a, b, c) in self._orders():
                    m = (b + c, b)[s]
                    self._add(p, chips[m], rb1, p, s)
                    self._pass(p, chips[m], 5 + s, b, rb2, p, s)

        def p2b(self):
            for s in (2, 3):
                self._got(1 + s)
                for p, (a, b, c) in self._orders():
                    self._add(p, chips[(c, 0)[s - 2]], rb1, p, s)

        def p3(self):
            self._got(5)
            for p, (a, b, c) in self._orders():
                self._add(p, chips[c], rb2, p, 0)
                self._pass(p, chips[c], 7, c, rb3, p)
            self._got(6)
            for p, (a, b, c) in self._orders():
                self._add(p, chips[0], rb2, p, 1)

        def p4(self):
            self._got(7)
            for p in range(3):
                rows = self.rows(p, chips[0])
                grads[rows, :] = S[rows, :] + self._buf(rb3, p)[...]
            self.start()

    class Push:
        def __init__(self, buf):
            self.buf, self.ssem, self.rsem = buf, new_sems(0, 1), new_sems(1, 1)

        def start(self):
            for i in range(1, NDEV):
                send(self.buf.at[me], self.buf.at[me], self.ssem, self.rsem, lax.rem(me + i, NDEV))

        def wait(self):
            arrived(self.buf.at[pl.ds(0, NDEV - 1)], self.rsem)

        def finish(self):
            sent(self.buf.at[pl.ds(0, NDEV - 1)], self.ssem)

    def order(i):
        return 4 - 2 * i + lax.div(i * (i - 1), 2)

    def device_of(slot):
        g = lax.div(slot + 1, 3)
        i = lax.rem(slot + 1, 3)
        near = order(i)
        m = jnp.where(slot < 2, 0, jnp.where(g < 3, near, jnp.where(g < 5, 7 - near, 7)))
        oth = jnp.where(slot < 2, slot, jnp.where(slot < 14, lax.rem(g - 1, 2), slot - 14))
        k = core + oth - 2 * core * oth
        return flip(m) * 2 + k

    def rowsl(q):
        return pl.ds(pl.multiple_of(q * R, R), R)

    def diag(r0, t):
        return (lax.broadcasted_iota(jnp.int32, (CH, L), 0) + r0
                == lax.broadcasted_iota(jnp.int32, (CH, L), 1) + L * t)

    def row_slot(slot, own):
        q = me if own else device_of(slot)
        s512 = dot(u_all[rowsl(me), :], v_all[rowsl(q), :], NT)
        for t in range(4):
            S[pl.ds(pl.multiple_of((slot * 4 + t) * R, R), R), :] = s512[:, L * t:L * t + L]

        def chunk(r, _):
            r0 = pl.multiple_of(r * CH, CH)
            rs = pl.ds(r0, CH)
            idc = idcol[rs, :]
            mo = m_ref[rs, :]
            vals = []
            pos = jnp.zeros((CH, L), F32)
            for t in range(4):
                off = pl.ds(pl.multiple_of((slot * 4 + t) * R + r0, CH), CH)
                s = S[off, :] * SCALE - lq_all[q, t:t + 1, :]
                hit = idc == ids_all[q, t:t + 1, :]
                if own:
                    dg = diag(r0, t)
                    pos = pos + jnp.where(dg, s, 0.0)
                    hit = jnp.logical_and(hit, jnp.logical_not(dg))
                s = jnp.where(hit, -jnp.inf, s)
                S[off, :] = s
                vals.append(s)
            if own:
                pos_ref[rs, :] = pos
            mn = jnp.maximum(jnp.maximum(mo, jnp.maximum(vals[0], vals[1])), jnp.maximum(vals[2], vals[3]))
            tot = l_ref[rs, :] * jnp.exp(mo - mn)
            for s in vals:
                tot = tot + jnp.exp(s - mn)
            l_ref[rs, :] = tot
            m_ref[rs, :] = mn
            return 0
        lax.fori_loop(0, R // CH, chunk, 0)

    def row_slots(a, b):
        lax.fori_loop(a, b, lambda s, c: (row_slot(s, False), c)[1], 0)

    def row_finish():
        m = m_ref[...]
        top = jnp.max(m, axis=1, keepdims=True)
        tot = jnp.sum(l_ref[...] * jnp.exp(m - top), axis=1, keepdims=True)
        inv = 1.0 / (tot * float(B))
        cost = top + jnp.log(tot) - jnp.sum(pos_ref[...], axis=1, keepdims=True)
        m_ref[...] = jnp.broadcast_to(top, (R, L))
        l_ref[...] = jnp.broadcast_to(inv, (R, L))
        lane = lax.broadcasted_iota(jnp.int32, (R, L), 1)
        pack = jnp.where(lane == 0, top, jnp.where(lane == 1, inv, jnp.where(lane == 2, cost, 0.0)))
        st_all[me] = pack.T[0:8, :]

    def du_slot(slot, own):
        q = me if own else device_of(slot)

        def chunk(r, _):
            r0 = pl.multiple_of(r * CH, CH)
            rs = pl.ds(r0, CH)
            mc = m_ref[rs, :]
            ic = l_ref[rs, :]
            for t in range(4):
                off = pl.ds(pl.multiple_of((slot * 4 + t) * R + r0, CH), CH)
                g = jnp.exp(S[off, :] - mc) * ic
                if own:
                    g = g - jnp.where(diag(r0, t), 1.0 / B, 0.0)
                G[rs, L * t:L * t + L] = g.astype(BF16)
            return 0
        lax.fori_loop(0, R // CH, chunk, 0)
        part = dot(G[...], v_all[rowsl(q), :])
        acc[...] = part if own else acc[...] + part

    def du_slots(a, b):
        lax.fori_loop(a, b, lambda s, c: (du_slot(s, False), c)[1], 0)

    def dv_slot(slot, own):
        q = me if own else device_of(slot)
        big[...] = dot(v_all[rowsl(me), :], u_all[rowsl(q), :], NT)

        def chunk(r, _):
            r0 = pl.multiple_of(r * CH, CH)
            rs = pl.ds(r0, CH)
            idc = idcol[rs, :]
            lqc = lqcol[rs, :]
            for t in range(4):
                cs = slice(L * t, L * t + L)
                s = big[rs, cs] * SCALE - lqc
                hit = idc == ids_all[q, t:t + 1, :]
                if own:
                    dg = diag(r0, t)
                    hit = jnp.logical_and(hit, jnp.logical_not(dg))
                g = jnp.exp(jnp.where(hit, -jnp.inf, s) - st_all[q, 0:1, cs]) * st_all[q, 1:2, cs]
                if own:
                    g = g - jnp.where(dg, 1.0 / B, 0.0)
                G[rs, cs] = g.astype(BF16)
            return 0
        lax.fori_loop(0, R // CH, chunk, 0)
        part = dot(G[...], u_all[rowsl(q), :])
        acc[...] = part if own else acc[...] + part

    def dv_slots(a, b):
        lax.fori_loop(a, b, lambda s, c: (dv_slot(s, False), c)[1], 0)

    def put(t, r0, val):
        n = val.shape[0]
        for p in range(3):
            S[pl.ds(pl.multiple_of(wrow(t, p, 0) + r0, 8), n), :] = val[:, L * p:L * p + L]

    def backward(t, reds, hooks):
        d = acc[...] * SCALE
        e = e_ref[t]
        inv = inv_ref[t]
        s = jnp.sum(e * d, axis=1, keepdims=True)
        dzb = ((d - e * s) * jnp.concatenate([inv, inv, inv], axis=1)).astype(BF16)
        g3 = dot(h2[t], dzb, TN)
        put(t, 2 * D, g3[:D // 2])
        put(t, HALF + 2 * D, g3[D // 2:])
        da2 = jnp.where(h2[t] > 0, dot(dzb, w3b[t], NT), 0.0).astype(BF16)
        G[:, 0:D] = da2

        def mid(i):
            c = lax.rem(i + 2 * (1 - core), 4)
            base = lax.div(c, 2) * HALF + lax.rem(c, 2) * SEG
            cols = pl.ds(pl.multiple_of(c * D, L), D)
            g2 = G[:, 0:D]
            put(t, base, dot(h1[t, :, cols], g2, TN))
            g1 = dot(g2, w2b[t, cols, :], NT)
            da1[...] = jnp.where(h1[t, :, cols] > 0, g1, 0.0).astype(BF16)
            put(t, base + D, dot(xb[t], da1[...], TN))

        hooks[0]()
        mid(0)
        hooks[1]()
        reds[0].cross()
        mid(1)
        hooks[2]()
        reds[1].cross()
        lax.fori_loop(2, 4, lambda i, x: (mid(i), x)[1], 0)

    pi, pq, ps = Push(ids_all), Push(lq_all), Push(st_all)
    ua, ub, ia, ib = Reduce(1, 0), Reduce(1, 1), Reduce(0, 0), Reduce(0, 1)

    def nothing():
        pass

    forward(0, v_all)
    pl.semaphore_wait(barrier, NDEV - 1)
    gv.start()
    pi.start()
    pq.start()
    forward(1, u_all)
    gv.f1()
    m_ref[...] = jnp.full((R, L), LOWEST, F32)
    l_ref[...] = jnp.zeros((R, L), F32)
    row_slot(0, True)
    pi.wait()
    pq.wait()
    gv.other(0)
    gv.f2()
    row_slots(1, 2)
    gv.f2b()
    row_slots(2, 5)
    gv.f3()
    gu.start()
    gv.other(1)
    row_slots(5, 8)
    gv.f4()
    row_slots(8, 11)
    gv.f5()
    gv.other(2)
    row_slots(11, 15)
    gv.other(3)
    row_slots(15, 16)
    row_finish()
    ps.start()
    gu.f1()
    gu.f2()
    du_slot(0, True)
    du_slots(1, 5)
    gu.f2b()
    du_slots(5, 10)
    gu.f3()
    du_slots(10, 16)
    backward(1, (ua, ub), (nothing, gu.f4, nothing))
    gu.f5()
    ua.p1()
    ps.wait()
    dv_slot(0, True)
    ub.p1()
    gu.other(0)
    gu.other(1)
    dv_slots(1, 4)
    ua.p2()
    gu.other(2)
    gu.other(3)
    dv_slots(4, 6)
    ua.p2b()
    dv_slots(6, 8)
    ub.p2()
    dv_slots(8, 10)
    ub.p2b()
    dv_slots(10, 12)
    ua.p3()
    dv_slots(12, 13)
    ub.p3()
    dv_slots(13, 14)
    ua.p4()
    dv_slots(14, 16)
    ub.p4()

    def turn(i):
        def go():
            (ua, ub)[i].f1()
            pl.semaphore_wait(ack.at[i], 1)
        return go

    backward(0, (ia, ib), (nothing, turn(0), turn(1)))
    ua.f2()
    ia.p1()
    ub.f2()
    ib.p1()
    ua.f2b()
    ua.f3()
    ia.p2()
    ub.f2b()
    ub.f3()
    ia.p2b()
    ib.p2()
    ib.p2b()
    ua.f4()
    ia.p3()
    ub.f4()
    ib.p3()
    ia.p4()
    ua.f5()
    ib.p4()
    ub.f5()
    total = jnp.sum(jnp.sum(st_all[...], axis=0)[2:3, :]) * (1.0 / B)
    loss[0, 0] = total
    ia.f1()
    ia.f2()
    ib.f1()
    ib.f2()
    ua.other()
    ub.other()
    ia.f2b()
    ia.f3()
    ib.f2b()
    ib.f3()
    ia.f4()
    ib.f4()
    ia.f5()
    ib.f5()
    ia.other()
    ib.other()
    for x in (gv, gu, pi, pq, ps, ua, ub, ia, ib):
        x.finish()


def write_kernel(loss_in, grads, loss, gu1, gu2, gu3, gi1, gi2, gi3, sem):
    loss[0, 0] = loss_in[0, 0]
    for t, (g1, g2, g3) in enumerate(((gi1, gi2, gi3), (gu1, gu2, gu3))):
        for p in range(3):
            pc = pl.ds(L * p, L)
            for h in range(2):
                o = t * WROWS + p * PACK + h * HALF
                jobs = [(o + 2 * D, g3.at[pl.ds(h * (D // 2), D // 2), pc])]
                for i in range(2):
                    c = 2 * h + i
                    jobs.append((o + i * SEG, g2.at[pl.ds(D * c, D), pc]))
                    jobs.append((o + i * SEG + D, g1.at[:, pl.ds(D * c + L * p, L)]))
                for r0, dst in jobs:
                    src = grads.at[pl.ds(r0, dst.shape[0]), :]
                    pltpu.make_async_copy(src, dst, sem).start()
    pltpu.make_async_copy(grads, grads, sem).wait()


def solution(mesh):
    vm = pl.BlockSpec(memory_space=pltpu.VMEM)
    sm = pl.BlockSpec(memory_space=pltpu.SMEM)
    hbm = pl.BlockSpec(memory_space=pl.ANY)
    shp = jax.ShapeDtypeStruct

    def device_step(user_x, item_x, item_id, log_q, user_w1, user_w2, user_w3, item_w1, item_w2, item_w3):
        V = pltpu.VMEM
        loss, grads = pl.pallas_call(
            kernel,
            out_shape=(shp((1, 1), F32), V((2 * WROWS, L), F32)),
            in_specs=[hbm, hbm, vm, vm] + [hbm] * 6,
            out_specs=(sm, vm),
            scratch_shapes=[
                V((64 * R, L), F32), V((B, D), BF16), V((B, D), BF16),
                V((2, R, D), BF16), V((2, R, H), BF16), V((2, R, D), BF16),
                V((2, R, D), F32), V((2, R, L), F32),
                V((2, D, H), BF16), V((2, H, D), BF16), V((2, D, D), BF16), V((R, D), BF16),
                V((NDEV, 4, L), jnp.int32), V((NDEV, 4, L), F32), V((NDEV, 8, R), F32),
                V((R, L), jnp.int32), V((R, L), F32), V((R, L), F32), V((R, L), F32), V((R, L), F32),
                V((R, R), BF16), V((R, D), F32), V((R, R), F32),
                V((3, HALF, L), F32), V((3, 4, BLK, L), F32), V((3, 2, BLK, L), F32),
                V((3, BLK, L), F32),
                pltpu.SemaphoreType.DMA((N_SEND,)), pltpu.SemaphoreType.DMA((N_RECV,)),
                pltpu.SemaphoreType.DMA((2, 6)), pltpu.SemaphoreType.REGULAR((2,)),
            ],
            compiler_params=pltpu.CompilerParams(collective_id=0, has_side_effects=True,
                                                 vmem_limit_bytes=VMEM_LIMIT),
            name='step',
        )(user_x, item_x, item_id.reshape(4, L), log_q.reshape(4, L),
          user_w1, user_w2, user_w3, item_w1, item_w2, item_w3)
        out = pl.pallas_call(
            write_kernel,
            out_shape=(shp((1, 1), F32), shp((D, H), F32), shp((H, D), F32), shp((D, D), F32),
                       shp((D, H), F32), shp((H, D), F32), shp((D, D), F32)),
            in_specs=[sm, vm],
            out_specs=(sm,) + (hbm,) * 6,
            scratch_shapes=[pltpu.SemaphoreType.DMA],
            compiler_params=pltpu.CompilerParams(vmem_limit_bytes=1 << 20),
            name='write',
        )(loss, grads)
        return (out[0].reshape(()),) + tuple(out[1:])

    batch_spec = P('dp', None)
    vec_spec = P('dp')
    whole = P()
    return jax.shard_map(device_step, mesh=mesh,
                         in_specs=(batch_spec, batch_spec, vec_spec, vec_spec, whole, whole, whole, whole, whole, whole),
                         out_specs=(whole,) * 7, check_vma=False)
```

time: 149 us -> 136 us (0.913)
  Pallas kernels: 148 us -> 135 us
    pallas_call x1, Pallas kernels: 143 us -> 130 us  [device_step(): pl.pallas_call(kernel, out_shape=(shp((1, 1), F32), V((2 * WROWS, L), F32...]
where the time goes in v3:
time: 136 us
  Pallas kernels  135 us (99%)
    pallas_call x1, Pallas kernels, device_step(): pl.pallas_call(kernel, out_shape=(shp((1, 1), F32), V((2 * WROWS, L), F32...  130 us
    pallas_call x1, Pallas kernels, device_step(): pl.pallas_call(write_kernel, out_shape=(shp((1, 1), F32), shp((D, H), F32...  5.07 us

profile of v3, /device:TPU:0, one launch (start us, length us, event | category | flops | bytes accessed | tf_op | source)
XLA Modules:
  0.0 135.9 jit_solution(2397407194602558622)
XLA Ops:
  0.6 130.0 %step.1 = (f32[1,1]{1,0:T(1,128)}, f32[20736,128]{1,0:T(8,128)S(1)}) custom-call(f32[512,384]{1,0:T(8,128)} %ux.1, f32[512,384]{1,0:T(8,128)} %ix.1, s32[4,128]{1,0:T(4,128)} %bitcast.3, f32[4,128]{1,0:T(4,128)} %bitcast.4, f32[384,1536]{1,0:T(8,128)} %uw1.1, f32[1536,384]{1,0:T(8,128)} %uw2.1, f32[384,384]{1,0:T(8,128)} %uw3.1, f32[384,1536]{1,0:T(8,128)} %iw1.1, ...), custom_call_target="tpu_custom_call" | custom-call | tf_op jit(solution)/shard_map/step/pallas_call | solution.py:628
  130.7 5.1 %write.1 = (f32[1,1]{1,0:T(1,128)}, f32[384,1536]{1,0:T(8,128)}, f32[1536,384]{1,0:T(8,128)}, f32[384,384]{1,0:T(8,128)}, f32[384,1536]{1,0:T(8,128)}, /*index=5*/f32[1536,384]{1,0:T(8,128)}, f32[384,384]{1,0:T(8,128)}) custom-call(f32[1,1]{1,0:T(1,128)} %get-tuple-element.16.loss_in, f32[20736,128]{1,0:T(8,128)S(1)} %get-tuple-element.17.grads), custom_call_target="tpu_custom_call" | custom-call | tf_op jit(solution)/shard_map/write/pallas_call | solution.py:651

commit v4 on v3

--- a/solution.py
+++ b/solution.py
@@ -343,21 +343,21 @@
         return (lax.broadcasted_iota(jnp.int32, (CH, L), 0) + r0
                 == lax.broadcasted_iota(jnp.int32, (CH, L), 1) + L * t)
 
-    def row_slot(slot, own):
-        q = me if own else device_of(slot)
-        s512 = dot(u_all[rowsl(me), :], v_all[rowsl(q), :], NT)
+    def row_dot(slot):
+        s512 = dot(u_all[rowsl(me), :], v_all[rowsl(device_of(slot)), :], NT)
         for t in range(4):
-            S[pl.ds(pl.multiple_of((slot * 4 + t) * R, R), R), :] = s512[:, L * t:L * t + L]
-
-        def chunk(r, _):
-            r0 = pl.multiple_of(r * CH, CH)
-            rs = pl.ds(r0, CH)
+            S[(slot * 4 + t) * R:(slot * 4 + t + 1) * R, :] = s512[:, L * t:L * t + L]
+
+    def row_rest(slot):
+        q = device_of(slot)
+        own = slot == 0
+        for r0 in range(0, R, CH):
+            rs = slice(r0, r0 + CH)
             idc = idcol[rs, :]
-            mo = m_ref[rs, :]
             vals = []
             pos = jnp.zeros((CH, L), F32)
             for t in range(4):
-                off = pl.ds(pl.multiple_of((slot * 4 + t) * R + r0, CH), CH)
+                off = slice((slot * 4 + t) * R + r0, (slot * 4 + t) * R + r0 + CH)
                 s = S[off, :] * SCALE - lq_all[q, t:t + 1, :]
                 hit = idc == ids_all[q, t:t + 1, :]
                 if own:
@@ -367,19 +367,26 @@
                 s = jnp.where(hit, -jnp.inf, s)
                 S[off, :] = s
                 vals.append(s)
+            mn = jnp.maximum(jnp.maximum(vals[0], vals[1]), jnp.maximum(vals[2], vals[3]))
             if own:
                 pos_ref[rs, :] = pos
-            mn = jnp.maximum(jnp.maximum(mo, jnp.maximum(vals[0], vals[1])), jnp.maximum(vals[2], vals[3]))
-            tot = l_ref[rs, :] * jnp.exp(mo - mn)
+                mn = jnp.maximum(mn, LOWEST)
+                tot = jnp.zeros((CH, L), F32)
+            else:
+                mo = m_ref[rs, :]
+                mn = jnp.maximum(mn, mo)
+                tot = l_ref[rs, :] * jnp.exp(mo - mn)
             for s in vals:
                 tot = tot + jnp.exp(s - mn)
             l_ref[rs, :] = tot
             m_ref[rs, :] = mn
-            return 0
-        lax.fori_loop(0, R // CH, chunk, 0)
 
     def row_slots(a, b):
-        lax.fori_loop(a, b, lambda s, c: (row_slot(s, False), c)[1], 0)
+        row_dot(a)
+        for slot in range(a, b):
+            if slot + 1 < b:
+                row_dot(slot + 1)
+            row_rest(slot)
 
     def row_finish():
         m = m_ref[...]
@@ -393,12 +400,9 @@
         pack = jnp.where(lane == 0, top, jnp.where(lane == 1, inv, jnp.where(lane == 2, cost, 0.0)))
         st_all[me] = pack.T[0:8, :]
 
-    def du_slot(slot, own):
-        q = me if own else device_of(slot)
-
-        def chunk(r, _):
-            r0 = pl.multiple_of(r * CH, CH)
-            rs = pl.ds(r0, CH)
+    def du_fill(slot, k, own=False):
+        for r0 in range(0, R, CH):
+            rs = slice(r0, r0 + CH)
             mc = m_ref[rs, :]
             ic = l_ref[rs, :]
             for t in range(4):
@@ -406,14 +410,19 @@
                 g = jnp.exp(S[off, :] - mc) * ic
                 if own:
                     g = g - jnp.where(diag(r0, t), 1.0 / B, 0.0)
-                G[rs, L * t:L * t + L] = g.astype(BF16)
-            return 0
-        lax.fori_loop(0, R // CH, chunk, 0)
-        part = dot(G[...], v_all[rowsl(q), :])
-        acc[...] = part if own else acc[...] + part
-
-    def du_slots(a, b):
-        lax.fori_loop(a, b, lambda s, c: (du_slot(s, False), c)[1], 0)
+                G[k, rs, L * t:L * t + L] = g.astype(BF16)
+
+    def du_dot(slot, k):
+        acc[...] += dot(G[k], v_all[rowsl(device_of(slot)), :])
+
+    def du_pairs(a, b):
+        def pair(i, x):
+            du_dot(2 * i, 0)
+            du_fill(2 * i + 1, 1)
+            du_dot(2 * i + 1, 1)
+            du_fill(2 * i + 2, 0)
+            return x
+        lax.fori_loop(a, b, pair, 0)
 
     def dv_slot(slot, own):
         q = me if own else device_of(slot)
@@ -434,10 +443,10 @@
                 g = jnp.exp(jnp.where(hit, -jnp.inf, s) - st_all[q, 0:1, cs]) * st_all[q, 1:2, cs]
                 if own:
                     g = g - jnp.where(dg, 1.0 / B, 0.0)
-                G[rs, cs] = g.astype(BF16)
+                G[0, rs, cs] = g.astype(BF16)
             return 0
         lax.fori_loop(0, R // CH, chunk, 0)
-        part = dot(G[...], u_all[rowsl(q), :])
+        part = dot(G[0], u_all[rowsl(q), :])
         acc[...] = part if own else acc[...] + part
 
     def dv_slots(a, b):
@@ -458,13 +467,13 @@
         put(t, 2 * D, g3[:D // 2])
         put(t, HALF + 2 * D, g3[D // 2:])
         da2 = jnp.where(h2[t] > 0, dot(dzb, w3b[t], NT), 0.0).astype(BF16)
-        G[:, 0:D] = da2
+        G[0, :, 0:D] = da2
 
         def mid(i):
             c = lax.rem(i + 2 * (1 - core), 4)
             base = lax.div(c, 2) * HALF + lax.rem(c, 2) * SEG
             cols = pl.ds(pl.multiple_of(c * D, L), D)
-            g2 = G[:, 0:D]
+            g2 = G[0, :, 0:D]
             put(t, base, dot(h1[t, :, cols], g2, TN))
             g1 = dot(g2, w2b[t, cols, :], NT)
             da1[...] = jnp.where(h1[t, :, cols] > 0, g1, 0.0).astype(BF16)
@@ -492,14 +501,11 @@
     pq.start()
     forward(1, u_all)
     gv.f1()
-    m_ref[...] = jnp.full((R, L), LOWEST, F32)
-    l_ref[...] = jnp.zeros((R, L), F32)
-    row_slot(0, True)
     pi.wait()
     pq.wait()
     gv.other(0)
+    row_slots(0, 2)
     gv.f2()
-    row_slots(1, 2)
     gv.f2b()
     row_slots(2, 5)
     gv.f3()
@@ -517,38 +523,42 @@
     ps.start()
     gu.f1()
     gu.f2()
-    du_slot(0, True)
-    du_slots(1, 5)
+    acc[...] = jnp.zeros((R, D), F32)
+    du_fill(0, 0, True)
+    du_pairs(0, 3)
     gu.f2b()
-    du_slots(5, 10)
-    gu.f3()
-    du_slots(10, 16)
-    backward(1, (ua, ub), (nothing, gu.f4, nothing))
-    gu.f5()
+    du_pairs(3, 7)
+    du_dot(14, 0)
+    du_fill(15, 1)
+    du_dot(15, 1)
+    backward(1, (ua, ub), (nothing, gu.f3, nothing))
     ua.p1()
+    gu.f4()
+    ub.p1()
     ps.wait()
-    dv_slot(0, True)
-    ub.p1()
     gu.other(0)
     gu.other(1)
+    dv_slot(0, True)
+    gu.f5()
     dv_slots(1, 4)
     ua.p2()
+    dv_slots(4, 6)
+    ua.p2b()
     gu.other(2)
     gu.other(3)
-    dv_slots(4, 6)
-    ua.p2b()
     dv_slots(6, 8)
     ub.p2()
-    dv_slots(8, 10)
+    dv_slots(8, 9)
     ub.p2b()
+    dv_slots(9, 10)
+    ua.p3()
     dv_slots(10, 12)
-    ua.p3()
+    ub.p3()
     dv_slots(12, 13)
-    ub.p3()
-    dv_slots(13, 14)
     ua.p4()
-    dv_slots(14, 16)
+    dv_slots(13, 15)
     ub.p4()
+    dv_slots(15, 16)
 
     def turn(i):
         def go():
@@ -637,7 +647,7 @@
                 V((2, D, H), BF16), V((2, H, D), BF16), V((2, D, D), BF16), V((R, D), BF16),
                 V((NDEV, 4, L), jnp.int32), V((NDEV, 4, L), F32), V((NDEV, 8, R), F32),
                 V((R, L), jnp.int32), V((R, L), F32), V((R, L), F32), V((R, L), F32), V((R, L), F32),
-                V((R, R), BF16), V((R, D), F32), V((R, R), F32),
+                V((2, R, R), BF16), V((R, D), F32), V((R, R), F32),
                 V((3, HALF, L), F32), V((3, 4, BLK, L), F32), V((3, 2, BLK, L), F32),
                 V((3, BLK, L), F32),
                 pltpu.SemaphoreType.DMA((N_SEND,)), pltpu.SemaphoreType.DMA((N_RECV,)),

time: 136 us -> 130 us (0.956)
  Pallas kernels: 135 us -> 129 us
    pallas_call x1, Pallas kernels: 130 us -> 124 us  [device_step(): pl.pallas_call(kernel, out_shape=(shp((1, 1), F32), V((2 * WROWS, L), F32...]
where the time goes in v4:
time: 130 us
  Pallas kernels  129 us (99%)
    pallas_call x1, Pallas kernels, device_step(): pl.pallas_call(kernel, out_shape=(shp((1, 1), F32), V((2 * WROWS, L), F32...  124 us
    pallas_call x1, Pallas kernels, device_step(): pl.pallas_call(write_kernel, out_shape=(shp((1, 1), F32), shp((D, H), F32...  5.07 us

profile of v4, /device:TPU:0, one launch (start us, length us, event | category | flops | bytes accessed | tf_op | source)
XLA Modules:
  0.0 129.6 jit_solution(3861517372515932838)
XLA Ops:
  0.6 123.7 %step.1 = (f32[1,1]{1,0:T(1,128)}, f32[20736,128]{1,0:T(8,128)S(1)}) custom-call(f32[512,384]{1,0:T(8,128)} %ux.1, f32[512,384]{1,0:T(8,128)} %ix.1, s32[4,128]{1,0:T(4,128)} %bitcast.3, f32[4,128]{1,0:T(4,128)} %bitcast.4, f32[384,1536]{1,0:T(8,128)} %uw1.1, f32[1536,384]{1,0:T(8,128)} %uw2.1, f32[384,384]{1,0:T(8,128)} %uw3.1, f32[384,1536]{1,0:T(8,128)} %iw1.1, ...), custom_call_target="tpu_custom_call" | custom-call | tf_op jit(solution)/shard_map/step/pallas_call | solution.py:638
  124.3 5.1 %write.1 = (f32[1,1]{1,0:T(1,128)}, f32[384,1536]{1,0:T(8,128)}, f32[1536,384]{1,0:T(8,128)}, f32[384,384]{1,0:T(8,128)}, f32[384,1536]{1,0:T(8,128)}, /*index=5*/f32[1536,384]{1,0:T(8,128)}, f32[384,384]{1,0:T(8,128)}) custom-call(f32[1,1]{1,0:T(1,128)} %get-tuple-element.16.loss_in, f32[20736,128]{1,0:T(8,128)S(1)} %get-tuple-element.17.grads), custom_call_target="tpu_custom_call" | custom-call | tf_op jit(solution)/shard_map/write/pallas_call | solution.py:661

commit v5 on v4

--- a/solution.py
+++ b/solution.py
@@ -38,7 +38,7 @@
            loss, grads,
            S, v_all, u_all, xb, h1, h2, e_ref, inv_ref, w1b, w2b, w3b, da1,
            ids_all, lq_all, st_all, idcol, lqcol, m_ref, l_ref, pos_ref, G, acc, big,
-           recv_d, rb1, rb2, rb3, send_sem, recv_sem, loc_sem, ack):
+           recv_d, rb1, rb2, rb3, send_sem, recv_sem, loc_sem, ack, hello):
     made = [0, 0]
 
     def new_sems(kind, n):
@@ -79,9 +79,19 @@
     def sent(ref, ssem):
         rc(ref, ref, ssem, 0, partner).wait_send()
 
+    near = [partner] + [nbr(d) for d in DIMS]
+
+    def greet(sem):
+        for n in near:
+            pl.semaphore_signal(sem, inc=1, device_id=(n,), device_id_type=MESH)
+
+    def greeted(i):
+        pl.semaphore_wait(hello.at[i], len(near))
+        if i < 2:
+            greet(hello.at[i + 1])
+
     barrier = pltpu.get_barrier_semaphore()
-    for i in range(1, NDEV):
-        pl.semaphore_signal(barrier, inc=1, device_id=(lax.rem(me + i, NDEV),), device_id_type=MESH)
+    greet(barrier)
 
     def load(src, dst, t, k):
         pltpu.make_async_copy(src, dst, loc_sem.at[t, k]).start()
@@ -91,7 +101,8 @@
         pltpu.make_async_copy(ref, ref, loc_sem.at[t, k]).wait()
 
     W2_AT, W3_AT, STAGE = 12 * D, 12 * D + 3 * H, WROWS + 3 * R
-    for t, (xr, w1, w2, w3) in enumerate(((ix, iw1, iw2, iw3), (ux, uw1, uw2, uw3))):
+
+    def start_loads(t, xr, w1, w2, w3):
         o = t * STAGE
 
         def columns(src, at, rows, c, k):
@@ -105,13 +116,18 @@
         for c in range(3):
             columns(w3, W3_AT, D, c, 5)
 
-    ids_all[me] = ids_in[...]
-    lq_all[me] = lq_in[...]
-    for t in range(4):
-        idcol[L * t:L * t + L, :] = jnp.broadcast_to(ids_in[t:t + 1, :], (L, L)).T
-        lqcol[L * t:L * t + L, :] = jnp.broadcast_to(lq_in[t:t + 1, :], (L, L)).T
-
-    def forward(t, dest):
+    start_loads(0, ix, iw1, iw2, iw3)
+    load(ids_in, ids_all.at[me], 0, 6)
+    load(lq_in, lq_all.at[me], 1, 6)
+
+    def columns_of_ids():
+        pltpu.make_async_copy(ids_in, ids_all.at[me], loc_sem.at[0, 6]).wait()
+        pltpu.make_async_copy(lq_in, lq_all.at[me], loc_sem.at[1, 6]).wait()
+        for t in range(4):
+            idcol[L * t:L * t + L, :] = jnp.broadcast_to(ids_all[me, t:t + 1, :], (L, L)).T
+            lqcol[L * t:L * t + L, :] = jnp.broadcast_to(lq_all[me, t:t + 1, :], (L, L)).T
+
+    def forward(t, dest, greeting):
         o = t * STAGE
 
         def take(dst, at, rows, c):
@@ -126,10 +142,16 @@
                 take(w1b, 0, D, 4 * n + c)
             cols = slice(4 * n * L, 4 * (n + 1) * L)
             h1[t, :, cols] = jnp.maximum(dot(xb[t], w1b[t, :, cols]), 0.0).astype(BF16)
+        if greeting:
+            greeted(0)
         loaded(t, 4, o + W2_AT, 3 * H)
+        if t == 0:
+            start_loads(1, ux, uw1, uw2, uw3)
         for c in range(3):
             take(w2b, W2_AT, H, c)
         h2[t] = jnp.maximum(dot(h1[t], w2b[t]), 0.0).astype(BF16)
+        if greeting:
+            greeted(1)
         loaded(t, 5, o + W3_AT, 3 * D)
         for c in range(3):
             take(w3b, W3_AT, D, c)
@@ -276,9 +298,15 @@
                     S[rows, :] += recv_d[p, self.at + q * self.blk:self.at + (q + 1) * self.blk, :]
             if self.t == 1:
                 pl.semaphore_signal(ack.at[self.piece], inc=1, device_id=(partner,), device_id_type=MESH)
-            for s in range(4):
+            self._first(0)
+
+        def _first(self, h):
+            for s in (2 * h, 2 * h + 1):
                 for p, (a, b, c) in self._orders():
                     self._pass(p, chips[a ^ (b + c, b, c, 0)[s]], 1 + s, a, rb1, p, s)
+
+        def p1b(self):
+            self._first(1)
 
         def p2(self):
             for s in range(2):
@@ -299,6 +327,8 @@
             for p, (a, b, c) in self._orders():
                 self._add(p, chips[c], rb2, p, 0)
                 self._pass(p, chips[c], 7, c, rb3, p)
+
+        def p3b(self):
             self._got(6)
             for p, (a, b, c) in self._orders():
                 self._add(p, chips[0], rb2, p, 1)
@@ -494,12 +524,15 @@
     def nothing():
         pass
 
-    forward(0, v_all)
-    pl.semaphore_wait(barrier, NDEV - 1)
+    forward(0, v_all, False)
+    pl.semaphore_wait(barrier, len(near))
     gv.start()
+    greet(hello.at[0])
+    columns_of_ids()
+    forward(1, u_all, True)
+    greeted(2)
     pi.start()
     pq.start()
-    forward(1, u_all)
     gv.f1()
     pi.wait()
     pq.wait()
@@ -533,56 +566,66 @@
     du_dot(15, 1)
     backward(1, (ua, ub), (nothing, gu.f3, nothing))
     ua.p1()
+    ua.p1b()
+    ub.p1()
     gu.f4()
-    ub.p1()
     ps.wait()
     gu.other(0)
     gu.other(1)
     dv_slot(0, True)
-    gu.f5()
     dv_slots(1, 4)
     ua.p2()
+    ub.p1b()
+    gu.f5()
     dv_slots(4, 6)
     ua.p2b()
     gu.other(2)
+    dv_slots(6, 9)
+    ua.p3()
+    ub.p2()
+    dv_slots(9, 10)
+    ua.p3b()
     gu.other(3)
-    dv_slots(6, 8)
-    ub.p2()
-    dv_slots(8, 9)
+    dv_slots(10, 11)
     ub.p2b()
-    dv_slots(9, 10)
-    ua.p3()
-    dv_slots(10, 12)
+    dv_slots(11, 12)
+    ua.p4()
+    dv_slots(12, 13)
     ub.p3()
-    dv_slots(12, 13)
-    ua.p4()
     dv_slots(13, 15)
+    ub.p3b()
+    dv_slots(15, 16)
     ub.p4()
-    dv_slots(15, 16)
 
     def turn(i):
         def go():
-            (ua, ub)[i].f1()
+            if i == 0:
+                ua.f1()
             pl.semaphore_wait(ack.at[i], 1)
         return go
 
     backward(0, (ia, ib), (nothing, turn(0), turn(1)))
     ua.f2()
     ia.p1()
+    ia.p1b()
+    ub.f1()
+    ib.p1()
+    ib.p1b()
+    ua.f2b()
+    ia.p2()
+    ua.f3()
     ub.f2()
-    ib.p1()
-    ua.f2b()
-    ua.f3()
-    ia.p2()
+    ia.p2b()
+    ib.p2()
     ub.f2b()
     ub.f3()
-    ia.p2b()
-    ib.p2()
     ib.p2b()
+    ia.p3()
     ua.f4()
-    ia.p3()
+    ia.p3b()
+    ib.p3()
     ub.f4()
-    ib.p3()
+    ib.p3b()
     ia.p4()
     ua.f5()
     ib.p4()
@@ -638,7 +681,7 @@
         loss, grads = pl.pallas_call(
             kernel,
             out_shape=(shp((1, 1), F32), V((2 * WROWS, L), F32)),
-            in_specs=[hbm, hbm, vm, vm] + [hbm] * 6,
+            in_specs=[hbm] * 10,
             out_specs=(sm, vm),
             scratch_shapes=[
                 V((64 * R, L), F32), V((B, D), BF16), V((B, D), BF16),
@@ -651,7 +694,8 @@
                 V((3, HALF, L), F32), V((3, 4, BLK, L), F32), V((3, 2, BLK, L), F32),
                 V((3, BLK, L), F32),
                 pltpu.SemaphoreType.DMA((N_SEND,)), pltpu.SemaphoreType.DMA((N_RECV,)),
-                pltpu.SemaphoreType.DMA((2, 6)), pltpu.SemaphoreType.REGULAR((2,)),
+                pltpu.SemaphoreType.DMA((2, 7)), pltpu.SemaphoreType.REGULAR((2,)),
+                pltpu.SemaphoreType.REGULAR((3,)),
             ],
             compiler_params=pltpu.CompilerParams(collective_id=0, has_side_effects=True,
                                                  vmem_limit_bytes=VMEM_LIMIT),

time: 130 us -> 129 us (level)
  no operation moved by 1% of the time
where the time goes in v5:
time: 129 us; the launch traced here: 128 us
  Pallas kernels  128 us (99%)
    pallas_call x1, Pallas kernels, device_step(): pl.pallas_call(kernel, out_shape=(shp((1, 1), F32), V((2 * WROWS, L), F32...  123 us
    pallas_call x1, Pallas kernels, device_step(): pl.pallas_call(write_kernel, out_shape=(shp((1, 1), F32), shp((D, H), F32...  5.07 us

profile of v5, /device:TPU:0, one launch (start us, length us, event | category | flops | bytes accessed | tf_op | source)
XLA Modules:
  0.0 128.4 jit_solution(2567015005109484969)
XLA Ops:
  0.6 122.5 %step.1 = (f32[1,1]{1,0:T(1,128)}, f32[20736,128]{1,0:T(8,128)S(1)}) custom-call(f32[512,384]{1,0:T(8,128)} %ux.1, f32[512,384]{1,0:T(8,128)} %ix.1, s32[4,128]{1,0:T(4,128)} %bitcast.3, f32[4,128]{1,0:T(4,128)} %bitcast.4, f32[384,1536]{1,0:T(8,128)} %uw1.1, f32[1536,384]{1,0:T(8,128)} %uw2.1, f32[384,384]{1,0:T(8,128)} %uw3.1, f32[384,1536]{1,0:T(8,128)} %iw1.1, ...), custom_call_target="tpu_custom_call" | custom-call | tf_op jit(solution)/shard_map/step/pallas_call | solution.py:681
  123.2 5.1 %write.1 = (f32[1,1]{1,0:T(1,128)}, f32[384,1536]{1,0:T(8,128)}, f32[1536,384]{1,0:T(8,128)}, f32[384,384]{1,0:T(8,128)}, f32[384,1536]{1,0:T(8,128)}, /*index=5*/f32[1536,384]{1,0:T(8,128)}, f32[384,384]{1,0:T(8,128)}) custom-call(f32[1,1]{1,0:T(1,128)} %get-tuple-element.16.loss_in, f32[20736,128]{1,0:T(8,128)S(1)} %get-tuple-element.17.grads), custom_call_target="tpu_custom_call" | custom-call | tf_op jit(solution)/shard_map/write/pallas_call | solution.py:705

commit v6 on v5

--- a/solution.py
+++ b/solution.py
@@ -193,10 +193,16 @@
             self._send(3, 2, ())
             self._cross(0)
 
-        def f1(self):
+        def f1w(self):
             self._wait(0)
+
+        def f1s(self):
             self._send(2, 1, (0,))
             self._send(4, 2, (0,))
+
+        def f1(self):
+            self.f1w()
+            self.f1s()
 
         def f2(self):
             self._wait(1)
@@ -552,9 +558,9 @@
     row_slots(11, 15)
     gv.other(3)
     row_slots(15, 16)
+    gu.f1()
     row_finish()
     ps.start()
-    gu.f1()
     gu.f2()
     acc[...] = jnp.zeros((R, D), F32)
     du_fill(0, 0, True)
@@ -605,30 +611,31 @@
         return go
 
     backward(0, (ia, ib), (nothing, turn(0), turn(1)))
-    ua.f2()
     ia.p1()
     ia.p1b()
-    ub.f1()
+    ub.f1w()
     ib.p1()
     ib.p1b()
+    ia.p2()
+    ib.p2()
+    ua.f2()
+    ia.p2b()
+    ia.p3()
+    ub.f1s()
+    ub.f2()
+    ib.p2b()
+    ia.p3b()
+    ib.p3()
     ua.f2b()
-    ia.p2()
     ua.f3()
-    ub.f2()
-    ia.p2b()
-    ib.p2()
+    ia.p4()
+    ib.p3b()
     ub.f2b()
     ub.f3()
-    ib.p2b()
-    ia.p3()
+    ib.p4()
     ua.f4()
-    ia.p3b()
-    ib.p3()
     ub.f4()
-    ib.p3b()
-    ia.p4()
     ua.f5()
-    ib.p4()
     ub.f5()
     total = jnp.sum(jnp.sum(st_all[...], axis=0)[2:3, :]) * (1.0 / B)
     loss[0, 0] = total

time: 129 us -> 128 us (level)
  no operation moved by 1% of the time
where the time goes in v6:
time: 128 us
  Pallas kernels  127 us (99%)
    pallas_call x1, Pallas kernels, device_step(): pl.pallas_call(kernel, out_shape=(shp((1, 1), F32), V((2 * WROWS, L), F32...  122 us
    pallas_call x1, Pallas kernels, device_step(): pl.pallas_call(write_kernel, out_shape=(shp((1, 1), F32), shp((D, H), F32...  5.07 us

profile of v6, /device:TPU:0, one launch (start us, length us, event | category | flops | bytes accessed | tf_op | source)
XLA Modules:
  0.0 128.0 jit_solution(2578301336627103942)
XLA Ops:
  0.6 122.1 %step.1 = (f32[1,1]{1,0:T(1,128)}, f32[20736,128]{1,0:T(8,128)S(1)}) custom-call(f32[512,384]{1,0:T(8,128)} %ux.1, f32[512,384]{1,0:T(8,128)} %ix.1, s32[4,128]{1,0:T(4,128)} %bitcast.3, f32[4,128]{1,0:T(4,128)} %bitcast.4, f32[384,1536]{1,0:T(8,128)} %uw1.1, f32[1536,384]{1,0:T(8,128)} %uw2.1, f32[384,384]{1,0:T(8,128)} %uw3.1, f32[384,1536]{1,0:T(8,128)} %iw1.1, ...), custom_call_target="tpu_custom_call" | custom-call | tf_op jit(solution)/shard_map/step/pallas_call | solution.py:688
  122.7 5.1 %write.1 = (f32[1,1]{1,0:T(1,128)}, f32[384,1536]{1,0:T(8,128)}, f32[1536,384]{1,0:T(8,128)}, f32[384,384]{1,0:T(8,128)}, f32[384,1536]{1,0:T(8,128)}, /*index=5*/f32[1536,384]{1,0:T(8,128)}, f32[384,384]{1,0:T(8,128)}) custom-call(f32[1,1]{1,0:T(1,128)} %get-tuple-element.16.loss_in, f32[20736,128]{1,0:T(8,128)S(1)} %get-tuple-element.17.grads), custom_call_target="tpu_custom_call" | custom-call | tf_op jit(solution)/shard_map/write/pallas_call | solution.py:712

commit v7 on v6

--- a/solution.py
+++ b/solution.py
@@ -14,7 +14,7 @@
 B = R * NDEV
 BLK = 216
 HALF = 8 * BLK
-N_SEND, N_RECV = 9, 89
+N_SEND, N_RECV = 9, 73
 PACK = 2 * HALF
 SEG = 960
 WROWS = 3 * PACK
@@ -250,13 +250,13 @@
         return t * WROWS + p * PACK + r
 
     class Reduce(Gather):
-        def __init__(self, t, piece):
+        def __init__(self, t, piece, other=None):
             self.t, self.piece = t, piece
             self.at, self.blk = ((0, SEG // 8), (SEG, (HALF - SEG) // 8))[piece]
             self.sub = (0, SEG // 8)[piece]
             super().__init__(lambda p, c: grads.at[self.rows(p, c), :], self._all_parts,
                              lambda n: grads.at[pl.ds(0, n * self.blk), :], new_sems(0, 1))
-            self.red = new_sems(1, 8)
+            self.red = new_sems(1, 8) if other is None else other.red
 
         def rows(self, p, c):
             return pl.ds(pl.multiple_of(wrow(self.t, p, 0) + core * HALF + self.at + c * self.blk, 8), self.blk)
@@ -525,7 +525,8 @@
         lax.fori_loop(2, 4, lambda i, x: (mid(i), x)[1], 0)
 
     pi, pq, ps = Push(ids_all), Push(lq_all), Push(st_all)
-    ua, ub, ia, ib = Reduce(1, 0), Reduce(1, 1), Reduce(0, 0), Reduce(0, 1)
+    ua, ub = Reduce(1, 0), Reduce(1, 1)
+    ia, ib = Reduce(0, 0, ua), Reduce(0, 1, ub)
 
     def nothing():
         pass

time: 128 us -> 128 us (level)
  no operation moved by 1% of the time
where the time goes in v7:
time: 128 us
  Pallas kernels  127 us (99%)
    pallas_call x1, Pallas kernels, device_step(): pl.pallas_call(kernel, out_shape=(shp((1, 1), F32), V((2 * WROWS, L), F32...  122 us
    pallas_call x1, Pallas kernels, device_step(): pl.pallas_call(write_kernel, out_shape=(shp((1, 1), F32), shp((D, H), F32...  5.07 us

profile of v7, /device:TPU:0, one launch (start us, length us, event | category | flops | bytes accessed | tf_op | source)
XLA Modules:
  0.0 127.9 jit_solution(10190900110002433580)
XLA Ops:
  0.6 122.0 %step.1 = (f32[1,1]{1,0:T(1,128)}, f32[20736,128]{1,0:T(8,128)S(1)}) custom-call(f32[512,384]{1,0:T(8,128)} %ux.1, f32[512,384]{1,0:T(8,128)} %ix.1, s32[4,128]{1,0:T(4,128)} %bitcast.3, f32[4,128]{1,0:T(4,128)} %bitcast.4, f32[384,1536]{1,0:T(8,128)} %uw1.1, f32[1536,384]{1,0:T(8,128)} %uw2.1, f32[384,384]{1,0:T(8,128)} %uw3.1, f32[384,1536]{1,0:T(8,128)} %iw1.1, ...), custom_call_target="tpu_custom_call" | custom-call | tf_op jit(solution)/shard_map/step/pallas_call | solution.py:689
  122.6 5.1 %write.1 = (f32[1,1]{1,0:T(1,128)}, f32[384,1536]{1,0:T(8,128)}, f32[1536,384]{1,0:T(8,128)}, f32[384,384]{1,0:T(8,128)}, f32[384,1536]{1,0:T(8,128)}, /*index=5*/f32[1536,384]{1,0:T(8,128)}, f32[384,384]{1,0:T(8,128)}) custom-call(f32[1,1]{1,0:T(1,128)} %get-tuple-element.16.loss_in, f32[20736,128]{1,0:T(8,128)S(1)} %get-tuple-element.17.grads), custom_call_target="tpu_custom_call" | custom-call | tf_op jit(solution)/shard_map/write/pallas_call | solution.py:713
